TPU v7x, 32 devices: a whole 2x2x4 slice. The times are simulated.
32 devices in a mesh: lon: 8 (over z, x), lat: 4 (over y, core).
Axes of the slice: x: 2, y: 2, z: 4, core: 2. Of those that a mesh axis runs over, the one named last changes fastest.
Arguments:
- thermal_anomaly: float32 [32, 64, 512], P(None, 'lon', 'lat'), may hold values from -5 to 5
- saltiness_anomaly: float32 [32, 64, 512], P(None, 'lon', 'lat'), may hold values from -5 to 5
- zonal_flow: float32 [32, 64, 512], P(None, 'lon', 'lat'), may hold values from -1.2 to 1.2
- meridional_flow: float32 [32, 64, 512], P(None, 'lon', 'lat'), may hold values from -1.2 to 1.2
- submerged_strata_number: int32 [64, 512], P('lon', 'lat'), may hold values from 1 to 32
- sea_indicator: int32 [64, 512], P('lon', 'lat'), may hold values 0 or 1
- strata_thickness: float32 [32], replicated, may hold values from 0.5 to 2
- earlier_sea_elevation: float32 [64, 512], P('lon', 'lat'), may hold values from -3 to 3
- sea_drive_term: float32 [64, 512], P('lon', 'lat'), may hold values from -10 to 10
Outputs:
- new_temperature: float32 [32, 64, 512], P(None, 'lon', 'lat')
- new_salinity: float32 [32, 64, 512], P(None, 'lon', 'lat')
- new_u_velocity: float32 [32, 64, 512], P(None, 'lon', 'lat')
- new_v_velocity: float32 [32, 64, 512], P(None, 'lon', 'lat')
- new_surface: float32 [64, 512], P('lon', 'lat')
- residual_rms: float32 [], replicated
All inputs are finite; a program needn't handle non-finite values. No bound on the sum of `sea_indicator` on one device may be relied on, other than what follows from the above.
Results may differ from a plain program's by a relative error of at most 0.0003.
Values sent between devices are 32-bit elements; how exact they have to be, the bound alone decides.
A program may use at most 128 MiB of HBM per device.

v0:
```python
import jax
import jax.numpy as jnp
from jax import lax
from jax.sharding import PartitionSpec as P

ITERS = 4


DIFFUSION = 0.15
MIXING = 0.1
EXPANSION = 0.2
CONTRACTION = 0.15
PRESSURE_SCALE = 0.02
CORIOLIS = 0.5
FRICTION = 0.01
DIVERGENCE = 0.3
STORAGE = 0.1
SPECTRUM_LOW = 0.1
SPECTRUM_HIGH = 1.9
GRAVITY = 0.3
EPSILON = 1e-06


def extended(x, sides, width, wrap):
    for axis, dim in sides:
        devices, length = (lax.axis_size(axis), x.shape[dim])
        up = [(i, (i + 1) % devices) for i in range(devices if wrap else devices - 1)]
        down = [(j, i) for i, j in up]
        last = lax.slice_in_dim(x, length - width, length, axis=dim)
        initial = lax.slice_in_dim(x, 0, width, axis=dim)
        before = lax.ppermute(last, axis, up)
        after = lax.ppermute(initial, axis, down)
        x = jnp.concatenate([before, x, after], axis=dim)
    return x


def from_partner(value, axis, bit):
    mask = 2**bit
    pairs = [(source, source ^ mask) for source in range(lax.axis_size(axis))]
    return lax.ppermute(value, axis, pairs)


def extend(field, sign_rows, width):
    meridian_points = field.shape[2]
    widened = extended(field, (("lat", 2),), width, False)
    top_rows = field[:, :, meridian_points - width :]
    partner_rows = top_rows
    for bit_index in range(lax.axis_size("lon").bit_length() - 1):
        partner_rows = from_partner(partner_rows, "lon", bit_index)
    mirrored = jnp.flip(partner_rows, 1)
    folded = jnp.flip(mirrored, 2) * sign_rows[:, None, None]
    at_pole = lax.axis_index("lat") == lax.axis_size("lat") - 1
    northern = jnp.where(at_pole, folded, widened[:, :, meridian_points + width :])
    widened = lax.dynamic_update_slice_in_dim(widened, northern, meridian_points + width, 2)
    return extended(widened, (("lon", 1),), width, True)


def center(field):
    return field[:, 1:-1, 1:-1]


def to_east(field):
    return field[:, 2:, 1:-1]


def to_west(field):
    return field[:, :-2, 1:-1]


def to_north(field):
    return field[:, 1:-1, 2:]


def to_south(field):
    return field[:, 1:-1, :-2]


def level_mask(strata_bottoms, strata_indices):
    level_index = jnp.arange(strata_indices).astype(strata_bottoms.dtype)[:, None, None]
    return jnp.where(level_index + 0.5 < strata_bottoms, 1.0, 0.0).astype(strata_bottoms.dtype)


def laplace(field, mask):
    middle = center(field)
    total = to_east(mask) * (to_east(field) - middle) + to_west(mask) * (to_west(field) - middle)
    total = (
        total
        + to_north(mask) * (to_north(field) - middle)
        + to_south(mask) * (to_south(field) - middle)
    )
    return center(mask) * total


def tracer_step(tracer, u_field, v_field, mask, thickness):
    middle = center(tracer)
    wet_mid = center(mask)
    u_mid = center(u_field)
    v_mid = center(v_field)
    flux_east = (
        wet_mid
        * to_east(mask)
        * (
            0.5 * (u_mid + to_east(u_field)) * 0.5 * (middle + to_east(tracer))
            - DIFFUSION * (to_east(tracer) - middle)
        )
    )
    flux_west = (
        wet_mid
        * to_west(mask)
        * (
            0.5 * (to_west(u_field) + u_mid) * 0.5 * (to_west(tracer) + middle)
            - DIFFUSION * (middle - to_west(tracer))
        )
    )
    flux_north = (
        wet_mid
        * to_north(mask)
        * (
            0.5 * (v_mid + to_north(v_field)) * 0.5 * (middle + to_north(tracer))
            - DIFFUSION * (to_north(tracer) - middle)
        )
    )
    flux_south = (
        wet_mid
        * to_south(mask)
        * (
            0.5 * (to_south(v_field) + v_mid) * 0.5 * (to_south(tracer) + middle)
            - DIFFUSION * (middle - to_south(tracer))
        )
    )
    horizontal = flux_west - flux_east + flux_south - flux_north
    spacing = 0.5 * (thickness[1:] + thickness[:-1])
    vflux = wet_mid[1:] * wet_mid[:-1] * (middle[1:] - middle[:-1]) / spacing[:, None, None]
    zero_plane = jnp.zeros_like(middle[:1])
    upper_flux = jnp.concatenate([vflux, zero_plane], axis=0)
    lower_flux = jnp.concatenate([zero_plane, vflux], axis=0)
    vertical = MIXING * (upper_flux - lower_flux) / thickness[:, None, None]
    return wet_mid * (middle + horizontal + vertical)


def pressure_gradients(temp_rim, salt_rim, mask, thickness):
    density = (CONTRACTION * salt_rim - EXPANSION * temp_rim) * thickness[:, None, None] * mask
    pressure = jnp.cumsum(density, axis=0)
    middle = center(pressure)
    wet_mid = center(mask)
    grad_x = (
        0.5
        * wet_mid
        * (
            to_east(mask) * (to_east(pressure) - middle)
            + to_west(mask) * (middle - to_west(pressure))
        )
    )
    grad_y = (
        0.5
        * wet_mid
        * (
            to_north(mask) * (to_north(pressure) - middle)
            + to_south(mask) * (middle - to_south(pressure))
        )
    )
    return (grad_x, grad_y)


def baroclinic(narrow, mask_narrow, lap_u, lap_v, thickness, coriolis, strata_indices):
    temp_rim = narrow[:strata_indices]
    salt_rim = narrow[strata_indices : 2 * strata_indices]
    u_rim = narrow[2 * strata_indices : 3 * strata_indices]
    v_rim = narrow[3 * strata_indices : 4 * strata_indices]
    new_temp = tracer_step(temp_rim, u_rim, v_rim, mask_narrow, thickness)
    new_salt = tracer_step(salt_rim, u_rim, v_rim, mask_narrow, thickness)
    grad_x, grad_y = pressure_gradients(temp_rim, salt_rim, mask_narrow, thickness)
    friction_u = laplace(lap_u, mask_narrow)
    friction_v = laplace(lap_v, mask_narrow)
    wet_mid = center(mask_narrow)
    u_mid = center(u_rim)
    v_mid = center(v_rim)
    u_star = wet_mid * (u_mid + coriolis * v_mid - PRESSURE_SCALE * grad_x - FRICTION * friction_u)
    v_star = wet_mid * (v_mid - coriolis * u_mid - PRESSURE_SCALE * grad_y - FRICTION * friction_v)
    height = jnp.sum(thickness[:, None, None] * mask_narrow, axis=0, keepdims=True)
    return (new_temp, new_salt, u_star, v_star, height, wet_mid)


def solver_weights(height, strata_indices):
    middle = center(height)
    w_east = jnp.minimum(middle, to_east(height)) / strata_indices
    w_west = jnp.minimum(middle, to_west(height)) / strata_indices
    w_north = jnp.minimum(middle, to_north(height)) / strata_indices
    w_south = jnp.minimum(middle, to_south(height)) / strata_indices
    diagonal = STORAGE + w_east + w_west + w_north + w_south
    return (w_east, w_west, w_north, w_south, diagonal)


def apply_operator(weights, field_rim):
    w_east, w_west, w_north, w_south, diagonal = weights
    coupled = (
        w_east * to_east(field_rim)
        + w_west * to_west(field_rim)
        + w_north * to_north(field_rim)
        + w_south * to_south(field_rim)
    )
    return diagonal * center(field_rim) - coupled


def line_factor(w_west, w_east, diagonal):
    count = diagonal.shape[0]
    position = jnp.arange(count).reshape((count,) + (1,) * (diagonal.ndim - 1))
    lower_band = jnp.where(position > 0, -w_west, 0.0)
    upper_band = jnp.where(position < count - 1, -w_east, 0.0)

    def forward(previous, inputs):
        lower_row, diag_row, upper_row = inputs
        inverse = 1.0 / (diag_row - lower_row * previous)
        factor = upper_row * inverse
        return (factor, (factor, inverse))

    _, (factors, pivots) = lax.scan(
        forward, jnp.zeros_like(diagonal[0]), (lower_band, diagonal, upper_band)
    )
    return (lower_band, factors, pivots)


def line_solve(lower_band, factors, pivots, values):

    def forward(previous, inputs):
        lower_row, inverse, value_row = inputs
        current = (value_row - lower_row * previous) * inverse
        return (current, current)

    _, partial_rows = lax.scan(forward, jnp.zeros_like(values[0]), (lower_band, pivots, values))

    def backward(following, inputs):
        factor, partial_row = inputs
        current = partial_row - factor * following
        return (current, current)

    _, solved = lax.scan(backward, jnp.zeros_like(values[0]), (factors, partial_rows), reverse=True)
    return solved


def global_rms(residual, cells):
    total = lax.psum(jnp.sum(residual * residual), ("lon", "lat"))
    return jnp.sqrt(total / cells + EPSILON)


def per_device(
    thermal_anomaly,
    saltiness_anomaly,
    zonal_flow,
    meridional_flow,
    submerged_strata_number,
    sea_indicator,
    strata_thickness,
    earlier_sea_elevation,
    sea_drive_term,
):
    strata_indices = thermal_anomaly.shape[0]
    station_indices = thermal_anomaly.shape[1]
    meridian_points = thermal_anomaly.shape[2]
    real_number_kind = thermal_anomaly.dtype
    wet_surface = sea_indicator.astype(real_number_kind)
    strata_bottoms = (submerged_strata_number * sea_indicator).astype(real_number_kind)[None]
    joined_tracers = jnp.concatenate(
        [thermal_anomaly, saltiness_anomaly, zonal_flow, meridional_flow, strata_bottoms], axis=0
    )
    sign_rows = jnp.concatenate(
        [
            jnp.ones(2 * strata_indices, real_number_kind),
            -jnp.ones(2 * strata_indices, real_number_kind),
            jnp.ones(1, real_number_kind),
        ]
    )
    narrow = extend(joined_tracers, sign_rows, 1)
    mask_narrow = level_mask(narrow[4 * strata_indices :], strata_indices)
    inner_u = laplace(narrow[2 * strata_indices : 3 * strata_indices], mask_narrow)
    inner_v = laplace(narrow[3 * strata_indices : 4 * strata_indices], mask_narrow)
    lap_rim = extend(
        jnp.concatenate([inner_u, inner_v], axis=0),
        -jnp.ones(2 * strata_indices, real_number_kind),
        1,
    )
    lap_u = lap_rim[:strata_indices]
    lap_v = lap_rim[strata_indices:]
    lat_index = (lax.axis_index("lat") * meridian_points + jnp.arange(meridian_points)).astype(
        real_number_kind
    )
    total_lat = lax.axis_size("lat") * meridian_points
    coriolis = CORIOLIS * (2.0 * (lat_index + 0.5) / total_lat - 1.0)
    new_temp, new_salt, u_star, v_star, height, wet_mid = baroclinic(
        narrow, mask_narrow, lap_u, lap_v, strata_thickness, coriolis, strata_indices
    )
    weights = solver_weights(height, strata_indices)
    lower_band, factors, pivots = line_factor(weights[1][0], weights[0][0], weights[4][0])

    def precondition(values):
        return line_solve(lower_band, factors, pivots, values[0])[None]

    transport_u = jnp.sum(strata_thickness[:, None, None] * u_star, axis=0, keepdims=True)
    transport_v = jnp.sum(strata_thickness[:, None, None] * v_star, axis=0, keepdims=True)
    start_field = (wet_surface * earlier_sea_elevation)[None]
    surface_signs = jnp.array([-1.0, -1.0, 1.0], real_number_kind)
    plus_one = jnp.ones(1, real_number_kind)
    moved = extend(
        jnp.concatenate([transport_u, transport_v, start_field], axis=0), surface_signs, 1
    )
    divergence = 0.5 * (to_east(moved[0:1]) - to_west(moved[0:1])) + 0.5 * (
        to_north(moved[1:2]) - to_south(moved[1:2])
    )
    right_side = wet_surface[None] * (sea_drive_term[None] - DIVERGENCE * divergence)
    solution = center(moved[2:3])
    residual = right_side - apply_operator(weights, moved[2:3])
    spectrum_mid = 0.5 * (SPECTRUM_HIGH + SPECTRUM_LOW)
    spectrum_half = 0.5 * (SPECTRUM_HIGH - SPECTRUM_LOW)
    spectrum_ratio = spectrum_mid / spectrum_half
    direction = precondition(residual) / spectrum_mid
    cheby_rho = 1.0 / spectrum_ratio
    for step_index in range(ITERS):
        solution = solution + direction
        if step_index + 1 < ITERS:
            residual = residual - apply_operator(weights, extend(direction, plus_one, 1))
        if step_index + 1 < ITERS:
            rho_next = 1.0 / (2.0 * spectrum_ratio - cheby_rho)
            direction = (
                rho_next * cheby_rho * direction
                + 2.0 * rho_next / spectrum_half * precondition(residual)
            )
            cheby_rho = rho_next
    cells = lax.axis_size("lon") * station_indices * lax.axis_size("lat") * meridian_points
    final_rim = extend(solution, plus_one, 1)
    residual_rms = global_rms(right_side - apply_operator(weights, final_rim), cells)
    slope_x = 0.5 * (to_east(final_rim) - to_west(final_rim))
    slope_y = 0.5 * (to_north(final_rim) - to_south(final_rim))
    new_u = wet_mid * (u_star - GRAVITY * slope_x)
    new_v = wet_mid * (v_star - GRAVITY * slope_y)
    return (new_temp, new_salt, new_u, new_v, solution[0], residual_rms)


def solution(mesh):
    return jax.shard_map(
        per_device,
        mesh=mesh,
        in_specs=(
            P(None, "lon", "lat"),
            P(None, "lon", "lat"),
            P(None, "lon", "lat"),
            P(None, "lon", "lat"),
            P("lon", "lat"),
            P("lon", "lat"),
            P(),
            P("lon", "lat"),
            P("lon", "lat"),
        ),
        out_specs=(
            P(None, "lon", "lat"),
            P(None, "lon", "lat"),
            P(None, "lon", "lat"),
            P(None, "lon", "lat"),
            P("lon", "lat"),
            P(),
        ),
        check_vma=False,
    )
```

profile of v0, /device:TPU:1, one launch (start us, length us, event | category | flops | bytes accessed | tf_op | source)
XLA Modules:
  0.0 243.0 jit_solution(18049223498466293871)
XLA Ops:
  7.7 4.0 %collective-permute-start = (f32[129,8,1]{0,1,2:T(8,128)S(1)}, f32[129,8,1]{0,1,2:T(8,128)S(1)}, u32[]{:S(2)}, u32[]{:S(2)}) collective-permute-start(f32[129,8,1]{0,1,2:T(8,128)S(1)} %copy.25), channel_id=1, source_target_pairs={{0,1},{1,2},{2,3},{4,5},{5,6},{6,7},{8,9},{9,10},{10,11},{12,13},{... | collective-permute-start | bytes 12392 | tf_op jit(solution)/shard_map/ppermute | solution.py:31
  21.3 13.6 %dynamic_update_slice.76 = f32[129,8,130]{2,1,0:T(8,128)S(1)} dynamic-update-slice(f32[129,8,130]{2,1,0:T(8,128)S(1)} %pad_maximum_fusion, f32[129,8,1]{2,1,0:T(8,128)S(1)} %copy.30, s32[]{:T(128)} %constant.261.clone.1, s32[]{:T(128)} %constant.261.clone.1, s32[]{:T(128)} %constant.262.clone.1) | dynamic-update-slice | bytes 8260 | tf_op jit(solution)/shard_map/dynamic_update_slice | solution.py:54
  35.4 3.9 %collective-permute-start.6 = (f32[129,1,130]{2,1,0:T(1,128)S(1)}, f32[129,1,130]{2,1,0:T(1,128)S(1)}, u32[]{:S(2)}, u32[]{:S(2)}) collective-permute-start(f32[129,1,130]{2,1,0:T(1,128)S(1)} %get-tuple-element.890), channel_id=1, source_target_pairs={{4,0},{8,4},{12,8},{16,12},{20,16},{24,20},{28,24},{0,28},{5,1},{9... | collective-permute-start | bytes 201248 | tf_op jit(solution)/shard_map/ppermute | solution.py:32
  39.3 3.6 %collective-permute-done.5 = f32[129,1,130]{2,1,0:T(1,128)S(1)} collective-permute-done((f32[129,1,130]{2,1,0:T(1,128)S(1)}, f32[129,1,130]{2,1,0:T(1,128)S(1)}, u32[]{:S(2)}, u32[]{:S(2)}) %collective-permute-start.5) | collective-permute-done | bytes 67112 | tf_op jit(solution)/shard_map/ppermute | solution.py:31
  45.3 5.1 %collective-permute-start.7 = (f32[64,8,1]{2,1,0:T(8,128)S(1)}, f32[64,8,1]{2,1,0:T(8,128)S(1)}, u32[]{:S(2)}, u32[]{:S(2)}) collective-permute-start(f32[64,8,1]{2,1,0:T(8,128)S(1)} %get-tuple-element.897), channel_id=1, source_target_pairs={{0,1},{1,2},{2,3},{4,5},{5,6},{6,7},{8,9},{9,10},{10,11},{12,13},{... | collective-permute-start | bytes 6152 | tf_op jit(solution)/shard_map/ppermute | solution.py:31
  54.2 5.4 %collective-permute-done.10 = f32[64,8,1]{2,1,0:T(8,128)S(1)} collective-permute-done((f32[64,8,1]{2,1,0:T(8,128)S(1)}, f32[64,8,1]{2,1,0:T(8,128)S(1)}, u32[]{:S(2)}, u32[]{:S(2)}) %collective-permute-start.10) | collective-permute-done | bytes 2080 | tf_op jit(solution)/shard_map/ppermute | solution.py:40
  62.7 10.4 %collective-permute-done.11 = f32[64,8,1]{2,1,0:T(8,128)S(1)} collective-permute-done((f32[64,8,1]{2,1,0:T(8,128)S(1)}, f32[64,8,1]{2,1,0:T(8,128)S(1)}, u32[]{:S(2)}, u32[]{:S(2)}) %collective-permute-start.11) | collective-permute-done | bytes 2080 | tf_op jit(solution)/shard_map/ppermute | solution.py:40
  74.8 4.7 %dynamic_update_slice.77 = f32[64,8,130]{2,1,0:T(8,128)S(1)} dynamic-update-slice(f32[64,8,130]{2,1,0:T(8,128)S(1)} %pad_maximum_fusion.4, f32[64,8,1]{2,1,0:T(8,128)S(1)} %multiply_select_fusion, s32[]{:T(128)} %constant.261.clone.1, s32[]{:T(128)} %constant.261.clone.1, s32[]{:T(128)} %constant.262.clone.1) | dynamic-update-slice | bytes 4100 | tf_op jit(solution)/shard_map/dynamic_update_slice | solution.py:54
  84.2 4.5 %collective-permute-done.13 = f32[64,1,130]{2,1,0:T(1,128)S(1)} collective-permute-done((f32[64,1,130]{2,1,0:T(1,128)S(1)}, f32[64,1,130]{2,1,0:T(1,128)S(1)}, u32[]{:S(2)}, u32[]{:S(2)}) %collective-permute-start.13) | collective-permute-done | bytes 33312 | tf_op jit(solution)/shard_map/ppermute | solution.py:31
  89.6 4.2 %collective-permute-start.14 = (f32[3,8,1]{2,1,0:T(8,128)S(1)}, f32[3,8,1]{2,1,0:T(8,128)S(1)}, u32[]{:S(2)}, u32[]{:S(2)}) collective-permute-start(f32[3,8,1]{2,1,0:T(8,128)S(1)} %get-tuple-element.903), channel_id=1, source_target_pairs={{0,1},{1,2},{2,3},{4,5},{5,6},{6,7},{8,9},{9,10},{10,11},{12,13},{... | collective-permute-start | bytes 296 | tf_op jit(solution)/shard_map/ppermute | solution.py:31
  93.9 4.5 %collective-permute-start.15 = (f32[3,8,1]{2,1,0:T(8,128)S(1)}, f32[3,8,1]{2,1,0:T(8,128)S(1)}, u32[]{:S(2)}, u32[]{:S(2)}) collective-permute-start(f32[3,8,1]{2,1,0:T(8,128)S(1)} %get-tuple-element.904), channel_id=1, source_target_pairs={{1,0},{2,1},{3,2},{5,4},{6,5},{7,6},{9,8},{10,9},{11,10},{13,12},{... | collective-permute-start | bytes 296 | tf_op jit(solution)/shard_map/ppermute | solution.py:32
  104.8 3.6 %collective-permute-done.20 = f32[3,1,130]{2,1,0:T(1,128)S(1)} collective-permute-done((f32[3,1,130]{2,1,0:T(1,128)S(1)}, f32[3,1,130]{2,1,0:T(1,128)S(1)}, u32[]{:S(2)}, u32[]{:S(2)}) %collective-permute-start.20) | collective-permute-done | bytes 1592 | tf_op jit(solution)/shard_map/ppermute | solution.py:31
  109.7 5.1 %collective-permute-start.21 = (f32[1,8,1]{2,1,0:T(8,128)S(1)}, f32[1,8,1]{2,1,0:T(8,128)S(1)}, u32[]{:S(2)}, u32[]{:S(2)}) collective-permute-start(f32[1,8,1]{2,1,0:T(8,128)S(1)} %get-tuple-element.921), channel_id=1, source_target_pairs={{0,1},{1,2},{2,3},{4,5},{5,6},{6,7},{8,9},{9,10},{10,11},{12,13},{... | collective-permute-start | bytes 104 | tf_op jit(solution)/shard_map/ppermute | solution.py:31
  119.9 3.3 %collective-permute-done.25 = f32[1,8,1]{2,1,0:T(8,128)S(1)} collective-permute-done((f32[1,8,1]{2,1,0:T(8,128)S(1)}, f32[1,8,1]{2,1,0:T(8,128)S(1)}, u32[]{:S(2)}, u32[]{:S(2)}) %collective-permute-start.25) | collective-permute-done | bytes 64 | tf_op jit(solution)/shard_map/ppermute | solution.py:40
  130.6 6.9 %collective-permute-start.28 = (f32[1,8,1]{2,1,0:T(8,128)S(1)}, f32[1,8,1]{2,1,0:T(8,128)S(1)}, u32[]{:S(2)}, u32[]{:S(2)}) collective-permute-start(f32[1,8,1]{2,1,0:T(8,128)S(1)} %get-tuple-element.919), channel_id=1, source_target_pairs={{0,1},{1,2},{2,3},{4,5},{5,6},{6,7},{8,9},{9,10},{10,11},{12,13},{... | collective-permute-start | bytes 104 | tf_op jit(solution)/shard_map/ppermute | solution.py:31
  142.5 3.4 %collective-permute-done.32 = f32[1,8,1]{2,1,0:T(8,128)S(1)} collective-permute-done((f32[1,8,1]{2,1,0:T(8,128)S(1)}, f32[1,8,1]{2,1,0:T(8,128)S(1)}, u32[]{:S(2)}, u32[]{:S(2)}) %collective-permute-start.32) | collective-permute-done | bytes 64 | tf_op jit(solution)/shard_map/ppermute | solution.py:40
  148.8 4.1 %collective-permute-done.34 = f32[1,1,130]{2,1,0:T(1,128)S(1)} collective-permute-done((f32[1,1,130]{2,1,0:T(1,128)S(1)}, f32[1,1,130]{2,1,0:T(1,128)S(1)}, u32[]{:S(2)}, u32[]{:S(2)}) %collective-permute-start.34) | collective-permute-done | bytes 552 | tf_op jit(solution)/shard_map/ppermute | solution.py:31
  154.2 6.5 %collective-permute-start.35 = (f32[1,8,1]{2,1,0:T(8,128)S(1)}, f32[1,8,1]{2,1,0:T(8,128)S(1)}, u32[]{:S(2)}, u32[]{:S(2)}) collective-permute-start(f32[1,8,1]{2,1,0:T(8,128)S(1)} %get-tuple-element.917), channel_id=1, source_target_pairs={{0,1},{1,2},{2,3},{4,5},{5,6},{6,7},{8,9},{9,10},{10,11},{12,13},{... | collective-permute-start | bytes 104 | tf_op jit(solution)/shard_map/ppermute | solution.py:31
  165.8 3.3 %collective-permute-done.39 = f32[1,8,1]{2,1,0:T(8,128)S(1)} collective-permute-done((f32[1,8,1]{2,1,0:T(8,128)S(1)}, f32[1,8,1]{2,1,0:T(8,128)S(1)}, u32[]{:S(2)}, u32[]{:S(2)}) %collective-permute-start.39) | collective-permute-done | bytes 64 | tf_op jit(solution)/shard_map/ppermute | solution.py:40
  172.0 3.4 %collective-permute-done.41 = f32[1,1,130]{2,1,0:T(1,128)S(1)} collective-permute-done((f32[1,1,130]{2,1,0:T(1,128)S(1)}, f32[1,1,130]{2,1,0:T(1,128)S(1)}, u32[]{:S(2)}, u32[]{:S(2)}) %collective-permute-start.41) | collective-permute-done | bytes 552 | tf_op jit(solution)/shard_map/ppermute | solution.py:31
  176.8 6.5 %collective-permute-start.42 = (f32[1,8,1]{2,1,0:T(8,128)S(1)}, f32[1,8,1]{2,1,0:T(8,128)S(1)}, u32[]{:S(2)}, u32[]{:S(2)}) collective-permute-start(f32[1,8,1]{2,1,0:T(8,128)S(1)} %get-tuple-element.915), channel_id=1, source_target_pairs={{0,1},{1,2},{2,3},{4,5},{5,6},{6,7},{8,9},{9,10},{10,11},{12,13},{... | collective-permute-start | bytes 104 | tf_op jit(solution)/shard_map/ppermute | solution.py:31
  188.3 3.3 %collective-permute-done.46 = f32[1,8,1]{2,1,0:T(8,128)S(1)} collective-permute-done((f32[1,8,1]{2,1,0:T(8,128)S(1)}, f32[1,8,1]{2,1,0:T(8,128)S(1)}, u32[]{:S(2)}, u32[]{:S(2)}) %collective-permute-start.46) | collective-permute-done | bytes 64 | tf_op jit(solution)/shard_map/ppermute | solution.py:40
  195.0 3.7 %collective-permute-done.48 = f32[1,1,130]{2,1,0:T(1,128)S(1)} collective-permute-done((f32[1,1,130]{2,1,0:T(1,128)S(1)}, f32[1,1,130]{2,1,0:T(1,128)S(1)}, u32[]{:S(2)}, u32[]{:S(2)}) %collective-permute-start.48) | collective-permute-done | bytes 552 | tf_op jit(solution)/shard_map/ppermute | solution.py:31
  200.7 39.6 %psum.7 = f32[]{:T(128)} all-reduce(f32[]{:T(128)} %fusion.113), channel_id=1, replica_groups=mesh['lon'=8,'lat'=4] {'lon','lat'}, use_global_device_ids=true, to_apply=%region_23.24 | all-reduce | flops 1 | bytes 8 | tf_op jit(solution)/shard_map/psum | solution.py:242
  (350 shorter events, 87.3 us)
Async XLA Ops:
  5.6 8.4 %collective-permute-start.2 = (f32[129,8,1]{0,1,2:T(8,128)S(1)}, f32[129,8,1]{0,1,2:T(8,128)S(1)}, u32[]{:S(2)}, u32[]{:S(2)}) collective-permute-start(f32[129,8,1]{0,1,2:T(8,128)S(1)} %copy.25), channel_id=1, source_target_pairs={{0,4},{4,0},{8,12},{12,8},{16,20},{20,16},{24,28},{28,24},{1,5},{5... | collective-permute-start | bytes 12392 | tf_op jit(solution)/shard_map/ppermute | solution.py:40
  7.7 7.7 %collective-permute-start = (f32[129,8,1]{0,1,2:T(8,128)S(1)}, f32[129,8,1]{0,1,2:T(8,128)S(1)}, u32[]{:S(2)}, u32[]{:S(2)}) collective-permute-start(f32[129,8,1]{0,1,2:T(8,128)S(1)} %copy.25), channel_id=1, source_target_pairs={{0,1},{1,2},{2,3},{4,5},{5,6},{6,7},{8,9},{9,10},{10,11},{12,13},{... | collective-permute-start | bytes 12392 | tf_op jit(solution)/shard_map/ppermute | solution.py:31
  35.1 7.8 %collective-permute-start.5 = (f32[129,1,130]{2,1,0:T(1,128)S(1)}, f32[129,1,130]{2,1,0:T(1,128)S(1)}, u32[]{:S(2)}, u32[]{:S(2)}) collective-permute-start(f32[129,1,130]{2,1,0:T(1,128)S(1)} %get-tuple-element.889), channel_id=1, source_target_pairs={{0,4},{4,8},{8,12},{12,16},{16,20},{20,24},{24,28},{28,0},{1,5},{5... | collective-permute-start | bytes 201248 | tf_op jit(solution)/shard_map/ppermute | solution.py:31
  35.4 8.6 %collective-permute-start.6 = (f32[129,1,130]{2,1,0:T(1,128)S(1)}, f32[129,1,130]{2,1,0:T(1,128)S(1)}, u32[]{:S(2)}, u32[]{:S(2)}) collective-permute-start(f32[129,1,130]{2,1,0:T(1,128)S(1)} %get-tuple-element.890), channel_id=1, source_target_pairs={{4,0},{8,4},{12,8},{16,12},{20,16},{24,20},{28,24},{0,28},{5,1},{9... | collective-permute-start | bytes 201248 | tf_op jit(solution)/shard_map/ppermute | solution.py:32
  45.2 7.7 %collective-permute-start.9 = (f32[64,8,1]{2,1,0:T(8,128)S(1)}, f32[64,8,1]{2,1,0:T(8,128)S(1)}, u32[]{:S(2)}, u32[]{:S(2)}) collective-permute-start(f32[64,8,1]{2,1,0:T(8,128)S(1)} %get-tuple-element.897), channel_id=1, source_target_pairs={{0,4},{4,0},{8,12},{12,8},{16,20},{20,16},{24,28},{28,24},{1,5},{5... | collective-permute-start | bytes 6152 | tf_op jit(solution)/shard_map/ppermute | solution.py:40
  45.3 17.1 %collective-permute-start.7 = (f32[64,8,1]{2,1,0:T(8,128)S(1)}, f32[64,8,1]{2,1,0:T(8,128)S(1)}, u32[]{:S(2)}, u32[]{:S(2)}) collective-permute-start(f32[64,8,1]{2,1,0:T(8,128)S(1)} %get-tuple-element.897), channel_id=1, source_target_pairs={{0,1},{1,2},{2,3},{4,5},{5,6},{6,7},{8,9},{9,10},{10,11},{12,13},{... | collective-permute-start | bytes 6152 | tf_op jit(solution)/shard_map/ppermute | solution.py:31
  50.9 11.5 %collective-permute-start.8 = (f32[64,8,1]{2,1,0:T(8,128)S(1)}, f32[64,8,1]{2,1,0:T(8,128)S(1)}, u32[]{:S(2)}, u32[]{:S(2)}) collective-permute-start(f32[64,8,1]{2,1,0:T(8,128)S(1)} %get-tuple-element.898), channel_id=1, source_target_pairs={{1,0},{2,1},{3,2},{5,4},{6,5},{7,6},{9,8},{10,9},{11,10},{13,12},{... | collective-permute-start | bytes 6152 | tf_op jit(solution)/shard_map/ppermute | solution.py:32
  52.8 6.9 %collective-permute-start.10 = (f32[64,8,1]{2,1,0:T(8,128)S(1)}, f32[64,8,1]{2,1,0:T(8,128)S(1)}, u32[]{:S(2)}, u32[]{:S(2)}) collective-permute-start(f32[64,8,1]{2,1,0:T(8,128)S(1)} %collective-permute-done.9), channel_id=1, source_target_pairs={{0,8},{4,12},{8,0},{12,4},{16,24},{20,28},{24,16},{28,20},{1,9},{5... | collective-permute-start | bytes 6152 | tf_op jit(solution)/shard_map/ppermute | solution.py:40
  59.7 13.4 %collective-permute-start.11 = (f32[64,8,1]{2,1,0:T(8,128)S(1)}, f32[64,8,1]{2,1,0:T(8,128)S(1)}, u32[]{:S(2)}, u32[]{:S(2)}) collective-permute-start(f32[64,8,1]{2,1,0:T(8,128)S(1)} %collective-permute-done.10), channel_id=1, source_target_pairs={{0,16},{4,20},{8,24},{12,28},{16,0},{20,4},{24,8},{28,12},{1,17},{... | collective-permute-start | bytes 6152 | tf_op jit(solution)/shard_map/ppermute | solution.py:40
  82.8 5.8 %collective-permute-start.13 = (f32[64,1,130]{2,1,0:T(1,128)S(1)}, f32[64,1,130]{2,1,0:T(1,128)S(1)}, u32[]{:S(2)}, u32[]{:S(2)}) collective-permute-start(f32[64,1,130]{2,1,0:T(1,128)S(1)} %get-tuple-element.896), channel_id=1, source_target_pairs={{0,4},{4,8},{8,12},{12,16},{16,20},{20,24},{24,28},{28,0},{1,5},{5... | collective-permute-start | bytes 99848 | tf_op jit(solution)/shard_map/ppermute | solution.py:31
  89.6 9.6 %collective-permute-start.14 = (f32[3,8,1]{2,1,0:T(8,128)S(1)}, f32[3,8,1]{2,1,0:T(8,128)S(1)}, u32[]{:S(2)}, u32[]{:S(2)}) collective-permute-start(f32[3,8,1]{2,1,0:T(8,128)S(1)} %get-tuple-element.903), channel_id=1, source_target_pairs={{0,1},{1,2},{2,3},{4,5},{5,6},{6,7},{8,9},{9,10},{10,11},{12,13},{... | collective-permute-start | bytes 296 | tf_op jit(solution)/shard_map/ppermute | solution.py:31
  93.9 5.3 %collective-permute-start.15 = (f32[3,8,1]{2,1,0:T(8,128)S(1)}, f32[3,8,1]{2,1,0:T(8,128)S(1)}, u32[]{:S(2)}, u32[]{:S(2)}) collective-permute-start(f32[3,8,1]{2,1,0:T(8,128)S(1)} %get-tuple-element.904), channel_id=1, source_target_pairs={{1,0},{2,1},{3,2},{5,4},{6,5},{7,6},{9,8},{10,9},{11,10},{13,12},{... | collective-permute-start | bytes 296 | tf_op jit(solution)/shard_map/ppermute | solution.py:32
  103.2 5.1 %collective-permute-start.20 = (f32[3,1,130]{2,1,0:T(1,128)S(1)}, f32[3,1,130]{2,1,0:T(1,128)S(1)}, u32[]{:S(2)}, u32[]{:S(2)}) collective-permute-start(f32[3,1,130]{2,1,0:T(1,128)S(1)} %get-tuple-element.900), channel_id=1, source_target_pairs={{0,4},{4,8},{8,12},{12,16},{16,20},{20,24},{24,28},{28,0},{1,5},{5... | collective-permute-start | bytes 4688 | tf_op jit(solution)/shard_map/ppermute | solution.py:31
  109.7 7.0 %collective-permute-start.23 = (f32[1,8,1]{2,1,0:T(8,128)S(1)}, f32[1,8,1]{2,1,0:T(8,128)S(1)}, u32[]{:S(2)}, u32[]{:S(2)}) collective-permute-start(f32[1,8,1]{2,1,0:T(8,128)S(1)} %get-tuple-element.921), channel_id=1, source_target_pairs={{0,4},{4,0},{8,12},{12,8},{16,20},{20,16},{24,28},{28,24},{1,5},{5... | collective-permute-start | bytes 104 | tf_op jit(solution)/shard_map/ppermute | solution.py:40
  109.7 10.0 %collective-permute-start.21 = (f32[1,8,1]{2,1,0:T(8,128)S(1)}, f32[1,8,1]{2,1,0:T(8,128)S(1)}, u32[]{:S(2)}, u32[]{:S(2)}) collective-permute-start(f32[1,8,1]{2,1,0:T(8,128)S(1)} %get-tuple-element.921), channel_id=1, source_target_pairs={{0,1},{1,2},{2,3},{4,5},{5,6},{6,7},{8,9},{9,10},{10,11},{12,13},{... | collective-permute-start | bytes 104 | tf_op jit(solution)/shard_map/ppermute | solution.py:31
  130.5 8.9 %collective-permute-start.30 = (f32[1,8,1]{2,1,0:T(8,128)S(1)}, f32[1,8,1]{2,1,0:T(8,128)S(1)}, u32[]{:S(2)}, u32[]{:S(2)}) collective-permute-start(f32[1,8,1]{2,1,0:T(8,128)S(1)} %get-tuple-element.919), channel_id=1, source_target_pairs={{0,4},{4,0},{8,12},{12,8},{16,20},{20,16},{24,28},{28,24},{1,5},{5... | collective-permute-start | bytes 104 | tf_op jit(solution)/shard_map/ppermute | solution.py:40
  130.6 11.9 %collective-permute-start.28 = (f32[1,8,1]{2,1,0:T(8,128)S(1)}, f32[1,8,1]{2,1,0:T(8,128)S(1)}, u32[]{:S(2)}, u32[]{:S(2)}) collective-permute-start(f32[1,8,1]{2,1,0:T(8,128)S(1)} %get-tuple-element.919), channel_id=1, source_target_pairs={{0,1},{1,2},{2,3},{4,5},{5,6},{6,7},{8,9},{9,10},{10,11},{12,13},{... | collective-permute-start | bytes 104 | tf_op jit(solution)/shard_map/ppermute | solution.py:31
  147.5 5.4 %collective-permute-start.34 = (f32[1,1,130]{2,1,0:T(1,128)S(1)}, f32[1,1,130]{2,1,0:T(1,128)S(1)}, u32[]{:S(2)}, u32[]{:S(2)}) collective-permute-start(f32[1,1,130]{2,1,0:T(1,128)S(1)} %get-tuple-element.912), channel_id=1, source_target_pairs={{0,4},{4,8},{8,12},{12,16},{16,20},{20,24},{24,28},{28,0},{1,5},{5... | collective-permute-start | bytes 1568 | tf_op jit(solution)/shard_map/ppermute | solution.py:31
  154.2 8.4 %collective-permute-start.37 = (f32[1,8,1]{2,1,0:T(8,128)S(1)}, f32[1,8,1]{2,1,0:T(8,128)S(1)}, u32[]{:S(2)}, u32[]{:S(2)}) collective-permute-start(f32[1,8,1]{2,1,0:T(8,128)S(1)} %get-tuple-element.917), channel_id=1, source_target_pairs={{0,4},{4,0},{8,12},{12,8},{16,20},{20,16},{24,28},{28,24},{1,5},{5... | collective-permute-start | bytes 104 | tf_op jit(solution)/shard_map/ppermute | solution.py:40
  154.2 11.4 %collective-permute-start.35 = (f32[1,8,1]{2,1,0:T(8,128)S(1)}, f32[1,8,1]{2,1,0:T(8,128)S(1)}, u32[]{:S(2)}, u32[]{:S(2)}) collective-permute-start(f32[1,8,1]{2,1,0:T(8,128)S(1)} %get-tuple-element.917), channel_id=1, source_target_pairs={{0,1},{1,2},{2,3},{4,5},{5,6},{6,7},{8,9},{9,10},{10,11},{12,13},{... | collective-permute-start | bytes 104 | tf_op jit(solution)/shard_map/ppermute | solution.py:31
  170.2 5.2 %collective-permute-start.41 = (f32[1,1,130]{2,1,0:T(1,128)S(1)}, f32[1,1,130]{2,1,0:T(1,128)S(1)}, u32[]{:S(2)}, u32[]{:S(2)}) collective-permute-start(f32[1,1,130]{2,1,0:T(1,128)S(1)} %get-tuple-element.910), channel_id=1, source_target_pairs={{0,4},{4,8},{8,12},{12,16},{16,20},{20,24},{24,28},{28,0},{1,5},{5... | collective-permute-start | bytes 1568 | tf_op jit(solution)/shard_map/ppermute | solution.py:31
  176.8 8.5 %collective-permute-start.44 = (f32[1,8,1]{2,1,0:T(8,128)S(1)}, f32[1,8,1]{2,1,0:T(8,128)S(1)}, u32[]{:S(2)}, u32[]{:S(2)}) collective-permute-start(f32[1,8,1]{2,1,0:T(8,128)S(1)} %get-tuple-element.915), channel_id=1, source_target_pairs={{0,4},{4,0},{8,12},{12,8},{16,20},{20,16},{24,28},{28,24},{1,5},{5... | collective-permute-start | bytes 104 | tf_op jit(solution)/shard_map/ppermute | solution.py:40
  176.8 11.5 %collective-permute-start.42 = (f32[1,8,1]{2,1,0:T(8,128)S(1)}, f32[1,8,1]{2,1,0:T(8,128)S(1)}, u32[]{:S(2)}, u32[]{:S(2)}) collective-permute-start(f32[1,8,1]{2,1,0:T(8,128)S(1)} %get-tuple-element.915), channel_id=1, source_target_pairs={{0,1},{1,2},{2,3},{4,5},{5,6},{6,7},{8,9},{9,10},{10,11},{12,13},{... | collective-permute-start | bytes 104 | tf_op jit(solution)/shard_map/ppermute | solution.py:31
  193.4 5.2 %collective-permute-start.48 = (f32[1,1,130]{2,1,0:T(1,128)S(1)}, f32[1,1,130]{2,1,0:T(1,128)S(1)}, u32[]{:S(2)}, u32[]{:S(2)}) collective-permute-start(f32[1,1,130]{2,1,0:T(1,128)S(1)} %get-tuple-element.907), channel_id=1, source_target_pairs={{0,4},{4,8},{8,12},{12,16},{16,20},{20,24},{24,28},{28,0},{1,5},{5... | collective-permute-start | bytes 1568 | tf_op jit(solution)/shard_map/ppermute | solution.py:31
  (32 other events, 186.2 us)
where the time goes:
time: 245 us; the launch traced here: 243 us
  starting transfers between devices  82.3 us (34%)
  waiting for transfers between devices  75.8 us (31%)
  blocking collectives  39.6 us (16%)
  local copies, waits for them, and re-layouts  28.9 us (12%)
  other arithmetic  11.9 us (5%)
  between operations  3.16 us (1%)
    ppermute x14, starting transfers between devices, extended(): before = lax.ppermute(last, axis, up)  42 us
    psum x1, blocking collectives, global_rms(): total = lax.psum(jnp.sum(residual * residual), ('lon', 'lat'))  39.6 us
    ppermute x21, waiting for transfers between devices, from_partner(): return lax.ppermute(value, axis, pairs)  32.5 us
    ppermute x14, starting transfers between devices, extended(): after = lax.ppermute(initial, axis, down)  29 us
    ppermute x14, waiting for transfers between devices, extended(): before = lax.ppermute(last, axis, up)  25.9 us
    dynamic_update_slice x7, local copies, waits for them, and re-layouts, extend(): lax.dynamic_update_slice_in_dim(widened, northern, meridian_points + widt...  18.9 us
    ppermute x14, waiting for transfers between devices, extended(): after = lax.ppermute(initial, axis, down)  17.4 us
    ppermute x21, starting transfers between devices, from_partner(): return lax.ppermute(value, axis, pairs)  11.3 us
  transfers between devices with their start and end apart: 49, of which 27 were waited for; matrix products, arithmetic and copies ran while one was open for 2% of the time, Pallas kernels for 0%

commit v1 on v0

v1 whole, which is shorter than its diff:
```python
import functools

import jax
import jax.numpy as jnp
from jax import lax
from jax.experimental import pallas as pl
from jax.experimental.pallas import tpu as pltpu
from jax.sharding import PartitionSpec as P

ITERS = 4
DIFFUSION = 0.15
MIXING = 0.1
EXPANSION = 0.2
CONTRACTION = 0.15
PRESSURE_SCALE = 0.02
CORIOLIS = 0.5
FRICTION = 0.01
DIVERGENCE = 0.3
STORAGE = 0.1
SPECTRUM_LOW = 0.1
SPECTRUM_HIGH = 1.9
GRAVITY = 0.3
EPSILON = 1e-06

MESH = pl.DeviceIdType.MESH
F32 = jnp.float32
SLOT_N, SLOT_NE, SLOT_NW, SLOT_S, SLOT_SE, SLOT_SW = range(6)
SEM_E, SEM_W = 6, 7
FIELDS = 5


def iota(shape, axis):
    return lax.broadcasted_iota(jnp.int32, shape, axis)


def flip_rows(x):
    n = x.shape[0]
    row = iota(x.shape, 0)
    bit = n // 2
    while bit:
        up = pltpu.roll(x, bit, 0)
        down = pltpu.roll(x, n - bit, 0)
        x = up if 2 * bit == n else jnp.where((row & bit) != 0, up, down)
        bit //= 2
    return x


def step_kernel(n_lon, n_lat, t_ref, s_ref, u_ref, v_ref, num_ref, sea_ref, thick_ref, eta_ref,
                drive_ref, ot_ref, os_ref, ou_ref, ov_ref, op_ref, epk, wpk, npk, spk, slot_e,
                slot_w, slots, rim, send_sem, recv_sem):
    K, NI, NJ = t_ref.shape
    p = lax.axis_index("lon")
    q = lax.axis_index("lat")
    east_dev = lax.rem(p + 1, n_lon)
    west_dev = lax.rem(p + n_lon - 1, n_lon)
    at_pole = q == n_lat - 1
    not_pole = q < n_lat - 1
    not_south = q > 0
    mirror = n_lon - 1 - p
    mirror_ne = lax.rem(2 * n_lon - 2 - p, n_lon)
    mirror_nw = lax.rem(2 * n_lon - p, n_lon)
    ne_remote = jnp.logical_or(not_pole, mirror_ne != p)
    nw_remote = jnp.logical_or(not_pole, mirror_nw != p)
    ne_self = jnp.logical_and(at_pole, mirror_ne == p)
    nw_self = jnp.logical_and(at_pole, mirror_nw == p)

    barrier = pltpu.get_barrier_semaphore()

    def greet(lon, lat):
        pl.semaphore_signal(barrier, inc=1, device_id={"lon": lon, "lat": lat}, device_id_type=MESH)

    greet(east_dev, q)
    greet(west_dev, q)

    @pl.when(not_south)
    def _():
        for lon in (p, east_dev, west_dev):
            greet(lon, q - 1)

    @pl.when(not_pole)
    def _():
        for lon in (p, east_dev, west_dev):
            greet(lon, q + 1)

    @pl.when(at_pole)
    def _():
        greet(mirror, q)

    @pl.when(jnp.logical_and(at_pole, mirror_ne != p))
    def _():
        greet(mirror_ne, q)

    @pl.when(jnp.logical_and(at_pole, mirror_nw != p))
    def _():
        greet(mirror_nw, q)

    sub = iota((NI, NJ), 0)
    lane = iota((NI, NJ), 1)
    depth = (num_ref[...] * sea_ref[...]).astype(F32)

    fields = (t_ref, s_ref, u_ref, v_ref)
    for pk, d1, d2 in ((epk, NI - 1, NI - 2), (wpk, 0, 1)):
        for f, ref in enumerate(fields):
            pk[f * K:(f + 1) * K, :] = ref[:, d1, :]
        pk[4 * K:5 * K, :] = u_ref[:, d2, :]
        pk[5 * K:6 * K, :] = v_ref[:, d2, :]
        pk[6 * K:6 * K + NI, :] = jnp.zeros((NI, NJ), F32)
        pk[6 * K:6 * K + 1, :] = depth[d1:d1 + 1, :]
        pk[6 * K + 1:6 * K + 2, :] = depth[d2:d2 + 1, :]

    n0 = jnp.zeros((NI, NJ), F32)
    s0 = jnp.zeros((NI, NJ), F32)
    n1 = jnp.zeros((NI, NJ), F32)
    s1 = jnp.zeros((NI, NJ), F32)

    def put(acc, x, source, target):
        moved = pltpu.roll(x, (target - source) % NJ, 1) if source != target else x
        return jnp.where(lane == target, moved, acc)

    for f, ref in enumerate(fields):
        for k in range(K):
            x = ref[k]
            target = f * K + k
            n0 = put(n0, x, NJ - 1, target)
            s0 = put(s0, x, 0, target)
            if f >= 2:
                n1 = put(n1, x, NJ - 2, target)
                s1 = put(s1, x, 1, target)
    n1 = put(put(n1, depth, NJ - 1, 0), depth, NJ - 2, 1)
    s1 = put(put(s1, depth, 0, 0), depth, 1, 1)
    npk[0] = n0
    npk[1] = n1
    spk[0] = s0
    spk[1] = s1

    peers = (3 + 2 * not_pole.astype(jnp.int32) + 3 * not_south.astype(jnp.int32)
             + at_pole.astype(jnp.int32) * ((mirror_ne != p).astype(jnp.int32) + (mirror_nw != p).astype(jnp.int32)))
    pl.semaphore_wait(barrier, peers)

    def copy(src, dst, lon, lat, out, into):
        return pltpu.make_async_remote_copy(
            src_ref=src, dst_ref=dst, send_sem=send_sem.at[out], recv_sem=recv_sem.at[into],
            device_id={"lon": lon, "lat": lat}, device_id_type=MESH)

    def edge(src, slot, lon, lat, out):
        return copy(src, slots.at[slot], lon, lat, out, slot)

    to_east = copy(epk, slot_w, east_dev, q, SEM_E, SEM_W)
    to_west = copy(wpk, slot_e, west_dev, q, SEM_W, SEM_E)
    to_east.start()
    to_west.start()

    @pl.when(not_south)
    def _():
        edge(spk, SLOT_N, p, q - 1, SLOT_S).start()
        edge(spk, SLOT_NW, east_dev, q - 1, SLOT_SE).start()
        edge(spk, SLOT_NE, west_dev, q - 1, SLOT_SW).start()

    @pl.when(not_pole)
    def _():
        edge(npk, SLOT_S, p, q + 1, SLOT_N).start()
        edge(npk, SLOT_SW, east_dev, q + 1, SLOT_NE).start()
        edge(npk, SLOT_SE, west_dev, q + 1, SLOT_NW).start()

    @pl.when(at_pole)
    def _():
        edge(npk, SLOT_N, mirror, q, SLOT_N).start()

    @pl.when(jnp.logical_and(at_pole, mirror_ne != p))
    def _():
        edge(npk, SLOT_NE, mirror_ne, q, SLOT_NE).start()

    @pl.when(jnp.logical_and(at_pole, mirror_nw != p))
    def _():
        edge(npk, SLOT_NW, mirror_nw, q, SLOT_NW).start()

    edge(npk, SLOT_N, p, q, SLOT_N).wait_recv()

    @pl.when(ne_remote)
    def _():
        edge(npk, SLOT_NE, p, q, SLOT_NE).wait_recv()

    @pl.when(nw_remote)
    def _():
        edge(npk, SLOT_NW, p, q, SLOT_NW).wait_recv()

    @pl.when(not_south)
    def _():
        for slot in (SLOT_S, SLOT_SE, SLOT_SW):
            edge(spk, slot, p, q, slot).wait_recv()

    sign = jnp.where(lane >= 2 * K, -1.0, 1.0).astype(F32)

    def northern(slot, own):
        out = []
        for i in range(2):
            x = slots[slot, i]
            if own is not None:
                x = jnp.where(own, npk[i], x)
            out.append(jnp.where(at_pole, flip_rows(x) * sign, x))
        return out

    def southern(slot):
        return [jnp.where(not_south, slots[slot, i], 0.0) for i in range(2)]

    pn0, pn1 = northern(SLOT_N, None)
    pne0, pne1 = northern(SLOT_NE, ne_self)
    pnw0, pnw1 = northern(SLOT_NW, nw_self)
    ps0, ps1 = southern(SLOT_S)
    pse0, pse1 = southern(SLOT_SE)
    psw0, psw1 = southern(SLOT_SW)

    def shift_e(x, row):
        return jnp.where(sub == NI - 1, row, pltpu.roll(x, NI - 1, 0))

    def shift_w(x, row):
        return jnp.where(sub == 0, row, pltpu.roll(x, 1, 0))

    level_l = (lane - K * (lane // K)).astype(F32) + 0.5

    def wet_l(d):
        return jnp.where(level_l < d, 1.0, 0.0)

    def spread(x, i):
        return jnp.broadcast_to(x[:, i:i + 1], (NI, NJ))

    def packed_lap(c0, c1, e0, e1, w0, w1, own, own_depth):
        d = spread(c1, 0)
        de = shift_e(d, jnp.broadcast_to(e1[0:1, 0:1], (NI, NJ)))
        dw = shift_w(d, jnp.broadcast_to(w1[NI - 1:NI, 0:1], (NI, NJ)))
        xe = shift_e(c0, jnp.broadcast_to(e0[0:1, :], (NI, NJ)))
        xw = shift_w(c0, jnp.broadcast_to(w0[NI - 1:NI, :], (NI, NJ)))
        total = wet_l(de) * (xe - c0) + wet_l(dw) * (xw - c0)
        total = total + wet_l(spread(c1, 1)) * (c1 - c0) + wet_l(own_depth) * (own - c0)
        return wet_l(d) * total

    lap_n = packed_lap(pn0, pn1, pne0, pne1, pnw0, pnw1, n0, spread(depth, NJ - 1))
    lap_s = packed_lap(ps0, ps1, pse0, pse1, psw0, psw1, s0, spread(depth, 0))
    rim[4, 0:NI, :] = lap_n
    rim[5, 0:NI, :] = lap_s
    rim[4, NI:2 * NI, :] = pn0
    rim[5, NI:2 * NI, :] = ps0

    to_east.wait_recv()
    to_west.wait_recv()

    level_r = iota((K, NJ), 0)
    lane_r = iota((K, NJ), 1)
    level_rf = level_r.astype(F32) + 0.5

    def wet_r(d):
        return jnp.where(level_rf < d, 1.0, 0.0)

    def wide(row):
        return jnp.broadcast_to(row, (K, NJ))

    for side, (slot, pk, d1, cn0, cn1, cs0, cs1) in enumerate((
            (slot_e, epk, NI - 1, pne0[0:1], pne1[0:1], pse0[0:1], pse1[0:1]),
            (slot_w, wpk, 0, pnw0[NI - 1:], pnw1[NI - 1:], psw0[NI - 1:], psw1[NI - 1:]))):
        d = wide(slot[6 * K:6 * K + 1, :])
        far = wet_r(wide(slot[6 * K + 1:6 * K + 2, :]))
        own = wet_r(wide(depth[d1:d1 + 1, :]))
        dn = jnp.where(lane_r == NJ - 1, jnp.broadcast_to(cn1[:, 0:1], (K, NJ)), pltpu.roll(d, NJ - 1, 1))
        ds = jnp.where(lane_r == 0, jnp.broadcast_to(cs1[:, 0:1], (K, NJ)), pltpu.roll(d, 1, 1))
        mid, mn, ms = wet_r(d), wet_r(dn), wet_r(ds)
        for i in range(2):
            f = 2 + i
            x = slot[f * K:(f + 1) * K, :]
            pick = lane_r == level_r + f * K
            cn = jnp.sum(jnp.where(pick, wide(cn0), 0.0), axis=1, keepdims=True)
            cs = jnp.sum(jnp.where(pick, wide(cs0), 0.0), axis=1, keepdims=True)
            xn = jnp.where(lane_r == NJ - 1, jnp.broadcast_to(cn, (K, NJ)), pltpu.roll(x, NJ - 1, 1))
            xs = jnp.where(lane_r == 0, jnp.broadcast_to(cs, (K, NJ)), pltpu.roll(x, 1, 1))
            total = far * (slot[(4 + i) * K:(5 + i) * K, :] - x) + own * (pk[f * K:(f + 1) * K, :] - x)
            total = total + mn * (xn - x) + ms * (xs - x)
            rim[2 * side + i] = mid * total

    def shift_n(x, packed, source):
        return jnp.where(lane == NJ - 1, pltpu.roll(packed, NJ - 1 - source, 1), pltpu.roll(x, NJ - 1, 1))

    def shift_s(x, packed, source):
        return jnp.where(lane == 0, pltpu.roll(packed, lax.rem(NJ - source, NJ), 1), pltpu.roll(x, 1, 1))

    depth_e = shift_e(depth, slot_e[6 * K:6 * K + 1, :])
    depth_w = shift_w(depth, slot_w[6 * K:6 * K + 1, :])
    depth_n = shift_n(depth, pn1, 0)
    depth_s = jnp.where(lane == 0, ps1, pltpu.roll(depth, 1, 1))
    both_e = jnp.minimum(depth, depth_e)
    both_w = jnp.minimum(depth, depth_w)
    both_n = jnp.minimum(depth, depth_n)
    both_s = jnp.minimum(depth, depth_s)
    lat_index = (q * NJ + lane).astype(F32)
    coriolis = CORIOLIS * (2.0 * (lat_index + 0.5) / (n_lat * NJ) - 1.0)

    zero = jnp.zeros((NI, NJ), F32)

    def level(k, carry):
        pc, pe, pw, pn_, ps_, flux_t, flux_s, tu, tv, height = carry
        kf = lax.convert_element_type(k, F32) + 0.5
        h = thick_ref[k]
        nxt = jnp.minimum(k + 1, K - 1)
        h_next = thick_ref[nxt]
        hv = jnp.full((NI, NJ), h, F32)
        inv_space = 1.0 / (0.5 * (hv + h_next))
        inv_h = MIXING / hv

        def wet(d):
            return jnp.where(d > kf, 1.0, 0.0)

        mc = wet(depth)
        me, mw, mn, ms = wet(both_e), wet(both_w), wet(both_n), wet(both_s)
        below = jnp.where(jnp.logical_and(depth > kf + 1.0, k < K - 1), inv_space, 0.0)
        pn0v = rim[4, NI:2 * NI, :]
        ps0v = rim[5, NI:2 * NI, :]
        lapn = rim[4, 0:NI, :]
        laps = rim[5, 0:NI, :]

        def around(ref, f):
            x = ref[k]
            row = pl.ds(f * K + k, 1)
            return (x, shift_e(x, slot_e[row, :]), shift_w(x, slot_w[row, :]),
                    shift_n(x, pn0v, f * K + k), shift_s(x, ps0v, f * K + k))

        t = around(t_ref, 0)
        s = around(s_ref, 1)
        u = around(u_ref, 2)
        v = around(v_ref, 3)
        ae = 0.25 * me * (u[0] + u[1])
        aw = 0.25 * mw * (u[0] + u[2])
        an = 0.25 * mn * (v[0] + v[3])
        as_ = 0.25 * ms * (v[0] + v[4])
        ge, gw, gn, gs = DIFFUSION * me, DIFFUSION * mw, DIFFUSION * mn, DIFFUSION * ms

        def tracer(x, ref, flux_above):
            c, e, w, n, so = x
            total = aw * (w + c) - gw * (c - w) - ae * (c + e) + ge * (e - c)
            total = total + as_ * (so + c) - gs * (c - so) - an * (c + n) + gn * (n - c)
            flux = below * (ref[nxt] - c)
            return mc * (c + total + inv_h * (flux - flux_above)), flux

        new_t, flux_t = tracer(t, t_ref, flux_t)
        new_s, flux_s = tracer(s, s_ref, flux_s)
        ot_ref[k] = new_t
        os_ref[k] = new_s
        pressures = []
        for i, (acc, d) in enumerate(((pc, depth), (pe, depth_e), (pw, depth_w), (pn_, depth_n), (ps_, depth_s))):
            density = CONTRACTION * s[i] - EXPANSION * t[i]
            pressures.append(acc + jnp.where(d > kf, density * h, 0.0))
        pc, pe, pw, pn_, ps_ = pressures
        grad_x = 0.5 * (me * (pe - pc) + mw * (pc - pw))
        grad_y = 0.5 * (mn * (pn_ - pc) + ms * (pc - ps_))

        def biharmonic(x, i):
            c, e, w, n, so = x
            lap = me * (e - c) + mw * (w - c) + mn * (n - c) + ms * (so - c)
            row = pl.ds(k, 1)
            le = shift_e(lap, rim[i, row, :])
            lw = shift_w(lap, rim[2 + i, row, :])
            source = (2 + i) * K + k
            ln = shift_n(lap, lapn, source)
            ls = shift_s(lap, laps, source)
            return me * (le - lap) + mw * (lw - lap) + mn * (ln - lap) + ms * (ls - lap)

        u_star = mc * (u[0] + coriolis * v[0] - PRESSURE_SCALE * grad_x - FRICTION * biharmonic(u, 0))
        v_star = mc * (v[0] - coriolis * u[0] - PRESSURE_SCALE * grad_y - FRICTION * biharmonic(v, 1))
        ou_ref[k] = u_star
        ov_ref[k] = v_star
        return (pc, pe, pw, pn_, ps_, flux_t, flux_s, tu + h * u_star, tv + h * v_star, height + h * mc)

    unroll = 4 if K % 4 == 0 else 1

    def group(g, carry):
        for i in range(unroll):
            carry = level(g * unroll + i, carry)
        return carry

    carry = lax.fori_loop(0, K // unroll, group, (zero,) * 10)
    op_ref[0] = carry[9]
    op_ref[1] = sea_ref[...].astype(F32) * eta_ref[...]
    op_ref[2] = drive_ref[...]
    op_ref[3] = carry[7]
    op_ref[4] = carry[8]

    to_east.wait_send()
    to_west.wait_send()

    @pl.when(not_south)
    def _():
        for out in (SLOT_S, SLOT_SE, SLOT_SW):
            edge(spk, SLOT_N, p, q, out).wait_send()

    edge(npk, SLOT_N, p, q, SLOT_N).wait_send()

    @pl.when(ne_remote)
    def _():
        edge(npk, SLOT_NE, p, q, SLOT_NE).wait_send()

    @pl.when(nw_remote)
    def _():
        edge(npk, SLOT_NW, p, q, SLOT_NW).wait_send()


def surface_solve(load, n_lon, n_lat, K, NI, NJ, cells):
    tiles = range(n_lat)
    lines = range(NI)
    lane = iota((n_lon, NJ), 1)

    def every(fn, *arrays):
        return [[fn(*(a[b][s] for a in arrays)) for s in lines] for b in tiles]

    def east(x):
        return [x[b][1:] + [pltpu.roll(x[b][0], n_lon - 1, 0)] for b in tiles]

    def west(x):
        return [[pltpu.roll(x[b][NI - 1], 1, 0)] + x[b][:-1] for b in tiles]

    def north(x, sign):
        out = []
        for b in tiles:
            row = []
            for s in lines:
                if b + 1 < n_lat:
                    beyond = pltpu.roll(x[b + 1][s], NJ - 1, 1)
                else:
                    beyond = flip_rows(x[b][NI - 1 - s])
                    beyond = -beyond if sign < 0 else beyond
                row.append(jnp.where(lane == NJ - 1, beyond, pltpu.roll(x[b][s], NJ - 1, 1)))
            out.append(row)
        return out

    def south(x):
        out = []
        for b in tiles:
            row = []
            for s in lines:
                beyond = pltpu.roll(x[b - 1][s], 1, 1) if b > 0 else 0.0
                row.append(jnp.where(lane == 0, beyond, pltpu.roll(x[b][s], 1, 1)))
            out.append(row)
        return out

    height = load(0)
    scale = lambda a, c: jnp.minimum(a, c) * (1.0 / K)
    w_e = every(scale, height, east(height))
    w_w = every(scale, height, west(height))
    w_n = every(scale, height, north(height, 1))
    w_s = every(scale, height, south(height))
    diag = every(lambda a, b, c, d: STORAGE + a + b + c + d, w_e, w_w, w_n, w_s)

    def apply(x):
        return every(
            lambda dg, c, we, e, ww, w, wn, n, ws, s: dg * c - (we * e + ww * w + wn * n + ws * s),
            diag, x, w_e, east(x), w_w, west(x), w_n, north(x, 1), w_s, south(x))

    factors = [[None] * NI for _ in tiles]
    pivots = [[None] * NI for _ in tiles]
    for b in tiles:
        for s in lines:
            pivot = diag[b][s]
            if s > 0:
                pivot = pivot + w_w[b][s] * factors[b][s - 1]
            pivots[b][s] = 1.0 / pivot
            factors[b][s] = -w_e[b][s] * pivots[b][s]

    def precondition(r):
        out = []
        for b in tiles:
            part = []
            for s in lines:
                value = r[b][s]
                if s > 0:
                    value = value + w_w[b][s] * part[s - 1]
                part.append(value * pivots[b][s])
            for s in range(NI - 2, -1, -1):
                part[s] = part[s] - factors[b][s] * part[s + 1]
            out.append(part)
        return out

    x = load(1)
    drive = load(2)
    t_u = load(3)
    t_v = load(4)
    right = every(
        lambda h, d, e, w, n, s: jnp.where(h > 0.0, d - DIVERGENCE * (0.5 * (e - w) + 0.5 * (n - s)), 0.0),
        height, drive, east(t_u), west(t_u), north(t_v, -1), south(t_v))
    residual = every(lambda a, b: a - b, right, apply(x))
    mid = 0.5 * (SPECTRUM_HIGH + SPECTRUM_LOW)
    half = 0.5 * (SPECTRUM_HIGH - SPECTRUM_LOW)
    ratio = mid / half
    direction = every(lambda a: a / mid, precondition(residual))
    rho = 1.0 / ratio
    for step in range(ITERS):
        x = every(lambda a, b: a + b, x, direction)
        residual = every(lambda a, b: a - b, residual, apply(direction))
        if step + 1 < ITERS:
            rho_next = 1.0 / (2.0 * ratio - rho)
            keep, gain = rho_next * rho, 2.0 * rho_next / half
            direction = every(lambda d, z: keep * d + gain * z, direction, precondition(residual))
            rho = rho_next
    squares = every(lambda a: a * a, residual)
    total = functools.reduce(lambda a, b: a + b, [squares[b][s] for b in tiles for s in lines])
    total = jnp.sum(jnp.sum(total, axis=1, keepdims=True), axis=0, keepdims=True)
    rms = jnp.sqrt(total / cells + EPSILON)
    slope_x = every(lambda e, w: 0.5 * (e - w), east(x), west(x))
    slope_y = every(lambda n, s: 0.5 * (n - s), north(x, 1), south(x))
    return x, slope_x, slope_y, rms


def solve_kernel(n_lon, n_lat, g_ref, us_ref, vs_ref, num_ref, sea_ref, ou_ref, ov_ref, ox_ref,
                 orms_ref, held):
    K, NI, NJ = us_ref.shape
    p = lax.axis_index("lon")
    q = lax.axis_index("lat")

    flat = g_ref.reshape(n_lat * n_lon * FIELDS * NI, NJ)

    def load(f):
        return [[flat[pl.ds((b * n_lon * FIELDS + f) * NI + s, n_lon, stride=FIELDS * NI), :]
                 for s in range(NI)] for b in range(n_lat)]

    x, slope_x, slope_y, rms = surface_solve(load, n_lon, n_lat, K, NI, NJ, n_lon * NI * n_lat * NJ)
    for i, field in enumerate((x, slope_x, slope_y)):
        for b in range(n_lat):
            for s in range(NI):
                held[i, b, pl.ds(s, n_lon, stride=NI), :] = field[b][s]
    orms_ref[0] = jnp.max(jnp.broadcast_to(rms, (8, 128)))
    mine = pl.ds(pl.multiple_of(p * NI, NI), NI)
    ox_ref[...] = held[0, q, mine, :]
    su = GRAVITY * held[1, q, mine, :]
    sv = GRAVITY * held[2, q, mine, :]
    depth = (num_ref[...] * sea_ref[...]).astype(F32)
    for k in range(K):
        wet = depth > k + 0.5
        ou_ref[k] = jnp.where(wet, us_ref[k] - su, 0.0)
        ov_ref[k] = jnp.where(wet, vs_ref[k] - sv, 0.0)


def per_device(n_lon, n_lat, temp, salt, u, v, num, sea, thick, eta, drive):
    K, NI, NJ = temp.shape
    vmem = pl.BlockSpec(memory_space=pltpu.VMEM)
    smem = pl.BlockSpec(memory_space=pltpu.SMEM)
    big = jax.ShapeDtypeStruct((K, NI, NJ), F32)
    new_t, new_s, u_star, v_star, packet = pl.pallas_call(
        functools.partial(step_kernel, n_lon, n_lat),
        out_shape=(big, big, big, big, jax.ShapeDtypeStruct((FIELDS, NI, NJ), F32)),
        in_specs=[vmem] * 6 + [smem] + [vmem] * 2,
        out_specs=(vmem,) * 5,
        scratch_shapes=[
            pltpu.VMEM((6 * K + NI, NJ), F32), pltpu.VMEM((6 * K + NI, NJ), F32),
            pltpu.VMEM((2, NI, NJ), F32), pltpu.VMEM((2, NI, NJ), F32),
            pltpu.VMEM((6 * K + NI, NJ), F32), pltpu.VMEM((6 * K + NI, NJ), F32),
            pltpu.VMEM((6, 2, NI, NJ), F32), pltpu.VMEM((6, K, NJ), F32),
            pltpu.SemaphoreType.DMA((8,)), pltpu.SemaphoreType.DMA((8,)),
        ],
        compiler_params=pltpu.CompilerParams(collective_id=0, has_side_effects=True),
        name="step",
    )(temp, salt, u, v, num, sea, thick, eta, drive)
    gathered = lax.all_gather(packet, ("lat", "lon")).reshape(n_lat, n_lon, FIELDS, NI, NJ)
    new_u, new_v, surface, rms = pl.pallas_call(
        functools.partial(solve_kernel, n_lon, n_lat),
        out_shape=(big, big, jax.ShapeDtypeStruct((NI, NJ), F32), jax.ShapeDtypeStruct((1,), F32)),
        in_specs=[vmem] * 5,
        out_specs=(vmem, vmem, vmem, smem),
        scratch_shapes=[pltpu.VMEM((3, n_lat, n_lon * NI, NJ), F32)],
        name="solve",
    )(gathered, u_star, v_star, num, sea)
    return new_t, new_s, new_u, new_v, surface, rms.reshape(())


def solution(mesh):
    n_lon, n_lat = mesh.shape["lon"], mesh.shape["lat"]
    spec3 = P(None, "lon", "lat")
    spec2 = P("lon", "lat")
    return jax.shard_map(
        functools.partial(per_device, n_lon, n_lat),
        mesh=mesh,
        in_specs=(spec3, spec3, spec3, spec3, spec2, spec2, P(), spec2, spec2),
        out_specs=(spec3, spec3, spec3, spec3, spec2, P()),
        check_vma=False,
    )
```

time: 245 us -> 96.7 us (0.39)
  the two profiles are of different devices: /device:TPU:1 before, /device:TPU:0 now
where the time goes in v1:
time: 96.7 us; the launch traced here: 96.5 us
  blocking collectives  76.3 us (79%)
  Pallas kernels  17.9 us (19%)
  local copies, waits for them, and re-layouts  1.6 us (2%)
    all_gather x1, blocking collectives, per_device(): lax.all_gather(packet, ('lat', 'lon')).reshape(n_lat, n_lon, FIELDS, NI, NJ)  76.3 us
    pallas_call x1, Pallas kernels, per_device(): pl.pallas_call(functools.partial(step_kernel, n_lon, n_lat), out_shape=(b...  14.9 us
    pallas_call x1, Pallas kernels, per_device(): pl.pallas_call(functools.partial(solve_kernel, n_lon, n_lat), out_shape=(...  3.02 us

profile of v1, /device:TPU:0, one launch (start us, length us, event | category | flops | bytes accessed | tf_op | source)
XLA Modules:
  0.0 96.5 jit_solution(1192937786815899728)
XLA Ops:
  0.6 14.9 %step.1 = (f32[32,8,128]{2,1,0:T(8,128)}, f32[32,8,128]{2,1,0:T(8,128)}, f32[32,8,128]{2,1,0:T(8,128)}, f32[32,8,128]{2,1,0:T(8,128)}, f32[5,8,128]{2,1,0:T(8,128)}) custom-call(f32[32,8,128]{2,1,0:T(8,128)} %t_ref.1, f32[32,8,128]{2,1,0:T(8,128)} %s_ref.1, f32[32,8,128]{2,1,0:T(8,128)} %u_ref.1, f32[32,8,128]{2,1,0:T(8,128)} %v_ref.1, s32[8,128]{1,0:T(8,128)} %num_ref.3, ...), custom_call_target="tpu_custom_call" | custom-call | tf_op jit(solution)/shard_map/step/pallas_call | solution.py:542
  15.5 76.3 %all-gather = f32[160,8,128]{2,1,0:T(8,128)} all-gather(f32[5,8,128]{2,1,0:T(8,128)} %get-tuple-element.17), channel_id=2, replica_groups=mesh['lon'=8,'lat'=4] {'lat','lon'}, dimensions={0}, use_global_device_ids=true | all-gather | bytes 675840 | tf_op jit(solution)/shard_map/all_gather | solution.py:557
  91.9 0.0 copy-start.1
  91.9 3.0 %solve.1 = (f32[32,8,128]{2,1,0:T(8,128)}, f32[32,8,128]{2,1,0:T(8,128)}, f32[8,128]{1,0:T(8,128)}, f32[1]{0:T(128)}) custom-call(f32[4,8,5,8,128]{4,3,2,1,0:T(8,128)} %bitcast.2, f32[32,8,128]{2,1,0:T(8,128)} %get-tuple-element.18.us_ref, f32[32,8,128]{2,1,0:T(8,128)} %get-tuple-element.19.vs_ref, s32[8,128]{1,0:T(8,128)} %num_ref.3, s32[8,128]{1,0:T(8,128)} %sea_ref.3), custom_call_target="tpu_custom_call" | custom-call | tf_op jit(solution)/shard_map/solve/pallas_call | solution.py:558
  94.9 0.0 copy-done.1
  94.9 0.0 copy-start
  94.9 0.7 copy.17
  95.6 0.3 copy-done
  95.9 0.7 copy.18
Async XLA Ops:
  91.9 3.0 %copy-start.1 = (f32[32,8,128]{2,1,0:T(8,128)S(1)}, f32[32,8,128]{2,1,0:T(8,128)}, u32[]{:S(2)}) copy-start(f32[32,8,128]{2,1,0:T(8,128)} %get-tuple-element.30) | copy-start | bytes 393220
  94.9 1.0 copy-start

commit v2 on v1

--- a/solution.py
+++ b/solution.py
@@ -26,7 +26,8 @@
 F32 = jnp.float32
 SLOT_N, SLOT_NE, SLOT_NW, SLOT_S, SLOT_SE, SLOT_SW = range(6)
 SEM_E, SEM_W = 6, 7
-FIELDS = 5
+EARLY = 3
+LATE = 2
 
 
 def iota(shape, axis):
@@ -46,8 +47,8 @@
 
 
 def step_kernel(n_lon, n_lat, t_ref, s_ref, u_ref, v_ref, num_ref, sea_ref, thick_ref, eta_ref,
-                drive_ref, ot_ref, os_ref, ou_ref, ov_ref, op_ref, epk, wpk, npk, spk, slot_e,
-                slot_w, slots, rim, send_sem, recv_sem):
+                drive_ref, ot_ref, os_ref, ou_ref, ov_ref, ox_ref, orms_ref, epk, wpk, npk, spk, slot_e,
+                slot_w, slots, rim, early, late, held, send_sem, recv_sem, cast_send, cast_recv):
     K, NI, NJ = t_ref.shape
     p = lax.axis_index("lon")
     q = lax.axis_index("lat")
@@ -94,9 +95,31 @@
     def _():
         greet(mirror_nw, q)
 
+    parity = lax.rem(q, 2)
+    partner = q + 1 - 2 * parity
+    n_half = n_lon * n_lat // 2
+    me_half = (q // 2) * n_lon + p
+
+    def half_peer(r):
+        other = lax.rem(me_half + r, n_half)
+        return lax.rem(other, n_lon), 2 * (other // n_lon) + parity
+
+    def greet_half(r, carry):
+        greet(*half_peer(r))
+        return carry
+
+    lax.fori_loop(1, n_half, greet_half, 0)
+    greet(p, partner)
+
     sub = iota((NI, NJ), 0)
     lane = iota((NI, NJ), 1)
     depth = (num_ref[...] * sea_ref[...]).astype(F32)
+    height = jnp.zeros((NI, NJ), F32)
+    for k in range(K):
+        height = height + jnp.where(depth > k + 0.5, thick_ref[k], 0.0)
+    early[parity, me_half, 0] = height
+    early[parity, me_half, 1] = sea_ref[...].astype(F32) * eta_ref[...]
+    early[parity, me_half, 2] = drive_ref[...]
 
     fields = (t_ref, s_ref, u_ref, v_ref)
     for pk, d1, d2 in ((epk, NI - 1, NI - 2), (wpk, 0, 1)):
@@ -133,7 +156,7 @@
     spk[0] = s0
     spk[1] = s1
 
-    peers = (3 + 2 * not_pole.astype(jnp.int32) + 3 * not_south.astype(jnp.int32)
+    peers = (3 + n_half + 2 * not_pole.astype(jnp.int32) + 3 * not_south.astype(jnp.int32)
              + at_pole.astype(jnp.int32) * ((mirror_ne != p).astype(jnp.int32) + (mirror_nw != p).astype(jnp.int32)))
     pl.semaphore_wait(barrier, peers)
 
@@ -173,6 +196,28 @@
     @pl.when(jnp.logical_and(at_pole, mirror_nw != p))
     def _():
         edge(npk, SLOT_NW, mirror_nw, q, SLOT_NW).start()
+
+    def cast(buf, which):
+        def send(r, carry):
+            lon, lat = half_peer(r)
+            mine = buf.at[parity, me_half]
+            pltpu.make_async_remote_copy(
+                src_ref=mine, dst_ref=mine, send_sem=cast_send.at[which], recv_sem=cast_recv.at[which],
+                device_id={"lon": lon, "lat": lat}, device_id_type=MESH).start()
+            return carry
+
+        lax.fori_loop(1, n_half, send, 0)
+
+    def cast_wait(buf, sem):
+        rest = buf.at[parity, pl.ds(0, n_half - 1)]
+        pltpu.make_async_copy(rest, rest, sem).wait()
+
+    def hand_over(buf, which):
+        return pltpu.make_async_remote_copy(
+            src_ref=buf.at[parity], dst_ref=buf.at[parity], send_sem=cast_send.at[which],
+            recv_sem=cast_recv.at[which], device_id={"lon": p, "lat": partner}, device_id_type=MESH)
+
+    cast(early, 0)
 
     edge(npk, SLOT_N, p, q, SLOT_N).wait_recv()
 
@@ -295,7 +340,7 @@
     zero = jnp.zeros((NI, NJ), F32)
 
     def level(k, carry):
-        pc, pe, pw, pn_, ps_, flux_t, flux_s, tu, tv, height = carry
+        pc, pe, pw, pn_, ps_, flux_t, flux_s, tu, tv = carry
         kf = lax.convert_element_type(k, F32) + 0.5
         h = thick_ref[k]
         nxt = jnp.minimum(k + 1, K - 1)
@@ -365,7 +410,7 @@
         v_star = mc * (v[0] - coriolis * u[0] - PRESSURE_SCALE * grad_y - FRICTION * biharmonic(v, 1))
         ou_ref[k] = u_star
         ov_ref[k] = v_star
-        return (pc, pe, pw, pn_, ps_, flux_t, flux_s, tu + h * u_star, tv + h * v_star, height + h * mc)
+        return (pc, pe, pw, pn_, ps_, flux_t, flux_s, tu + h * u_star, tv + h * v_star)
 
     unroll = 4 if K % 4 == 0 else 1
 
@@ -374,12 +419,52 @@
             carry = level(g * unroll + i, carry)
         return carry
 
-    carry = lax.fori_loop(0, K // unroll, group, (zero,) * 10)
-    op_ref[0] = carry[9]
-    op_ref[1] = sea_ref[...].astype(F32) * eta_ref[...]
-    op_ref[2] = drive_ref[...]
-    op_ref[3] = carry[7]
-    op_ref[4] = carry[8]
+    carry = lax.fori_loop(0, K // unroll, group, (zero,) * 9)
+    late[parity, me_half, 0] = carry[7]
+    late[parity, me_half, 1] = carry[8]
+    cast(late, 1)
+
+    cast_wait(early, cast_recv.at[0])
+    early_over = hand_over(early, 2)
+    early_over.start()
+    early_over.wait_recv()
+
+    def loader(buf, count):
+        flat = buf.reshape(2 * n_half * count * NI, NJ)
+
+        def load(f):
+            return [[flat[pl.ds((((b % 2) * n_half + (b // 2) * n_lon) * count + f) * NI + s, n_lon,
+                                stride=count * NI), :] for s in range(NI)] for b in range(n_lat)]
+
+        return load
+
+    def late_loader():
+        cast_wait(late, cast_recv.at[1])
+        late_over = hand_over(late, 3)
+        late_over.start()
+        late_over.wait_recv()
+        return loader(late, LATE)
+
+    x, slope_x, slope_y, rms = surface_solve(loader(early, EARLY), late_loader, n_lon, n_lat, K, NI, NJ,
+                                             n_lon * NI * n_lat * NJ)
+    for i, field in enumerate((x, slope_x, slope_y)):
+        for b in range(n_lat):
+            for s in range(NI):
+                held[i, b, pl.ds(s, n_lon, stride=NI), :] = field[b][s]
+    orms_ref[0] = jnp.max(jnp.broadcast_to(rms, (8, 128)))
+    block = pl.ds(pl.multiple_of(p * NI, NI), NI)
+    ox_ref[...] = held[0, q, block, :]
+    su = GRAVITY * held[1, q, block, :]
+    sv = GRAVITY * held[2, q, block, :]
+    for k in range(K):
+        wet = depth > k + 0.5
+        ou_ref[k] = jnp.where(wet, ou_ref[k] - su, 0.0)
+        ov_ref[k] = jnp.where(wet, ov_ref[k] - sv, 0.0)
+
+    cast_wait(early, cast_send.at[0])
+    cast_wait(late, cast_send.at[1])
+    early_over.wait_send()
+    hand_over(late, 3).wait_send()
 
     to_east.wait_send()
     to_west.wait_send()
@@ -400,7 +485,7 @@
         edge(npk, SLOT_NW, p, q, SLOT_NW).wait_send()
 
 
-def surface_solve(load, n_lon, n_lat, K, NI, NJ, cells):
+def surface_solve(load, load_late, n_lon, n_lat, K, NI, NJ, cells):
     tiles = range(n_lat)
     lines = range(NI)
     lane = iota((n_lon, NJ), 1)
@@ -477,12 +562,13 @@
 
     x = load(1)
     drive = load(2)
-    t_u = load(3)
-    t_v = load(4)
-    right = every(
-        lambda h, d, e, w, n, s: jnp.where(h > 0.0, d - DIVERGENCE * (0.5 * (e - w) + 0.5 * (n - s)), 0.0),
-        height, drive, east(t_u), west(t_u), north(t_v, -1), south(t_v))
-    residual = every(lambda a, b: a - b, right, apply(x))
+    start = every(lambda h, d, a: jnp.where(h > 0.0, d, 0.0) - a, height, drive, apply(x))
+    load = load_late()
+    t_u = load(0)
+    t_v = load(1)
+    residual = every(
+        lambda h, d, e, w, n, s: d - jnp.where(h > 0.0, 0.5 * DIVERGENCE * ((e - w) + (n - s)), 0.0),
+        height, start, east(t_u), west(t_u), north(t_v, -1), south(t_v))
     mid = 0.5 * (SPECTRUM_HIGH + SPECTRUM_LOW)
     half = 0.5 * (SPECTRUM_HIGH - SPECTRUM_LOW)
     ratio = mid / half
@@ -505,64 +591,31 @@
     return x, slope_x, slope_y, rms
 
 
-def solve_kernel(n_lon, n_lat, g_ref, us_ref, vs_ref, num_ref, sea_ref, ou_ref, ov_ref, ox_ref,
-                 orms_ref, held):
-    K, NI, NJ = us_ref.shape
-    p = lax.axis_index("lon")
-    q = lax.axis_index("lat")
-
-    flat = g_ref.reshape(n_lat * n_lon * FIELDS * NI, NJ)
-
-    def load(f):
-        return [[flat[pl.ds((b * n_lon * FIELDS + f) * NI + s, n_lon, stride=FIELDS * NI), :]
-                 for s in range(NI)] for b in range(n_lat)]
-
-    x, slope_x, slope_y, rms = surface_solve(load, n_lon, n_lat, K, NI, NJ, n_lon * NI * n_lat * NJ)
-    for i, field in enumerate((x, slope_x, slope_y)):
-        for b in range(n_lat):
-            for s in range(NI):
-                held[i, b, pl.ds(s, n_lon, stride=NI), :] = field[b][s]
-    orms_ref[0] = jnp.max(jnp.broadcast_to(rms, (8, 128)))
-    mine = pl.ds(pl.multiple_of(p * NI, NI), NI)
-    ox_ref[...] = held[0, q, mine, :]
-    su = GRAVITY * held[1, q, mine, :]
-    sv = GRAVITY * held[2, q, mine, :]
-    depth = (num_ref[...] * sea_ref[...]).astype(F32)
-    for k in range(K):
-        wet = depth > k + 0.5
-        ou_ref[k] = jnp.where(wet, us_ref[k] - su, 0.0)
-        ov_ref[k] = jnp.where(wet, vs_ref[k] - sv, 0.0)
-
-
 def per_device(n_lon, n_lat, temp, salt, u, v, num, sea, thick, eta, drive):
     K, NI, NJ = temp.shape
     vmem = pl.BlockSpec(memory_space=pltpu.VMEM)
     smem = pl.BlockSpec(memory_space=pltpu.SMEM)
     big = jax.ShapeDtypeStruct((K, NI, NJ), F32)
-    new_t, new_s, u_star, v_star, packet = pl.pallas_call(
+    n_half = n_lon * n_lat // 2
+    row_scratch = pltpu.VMEM((6 * K + NI, NJ), F32)
+    new_t, new_s, new_u, new_v, surface, rms = pl.pallas_call(
         functools.partial(step_kernel, n_lon, n_lat),
-        out_shape=(big, big, big, big, jax.ShapeDtypeStruct((FIELDS, NI, NJ), F32)),
+        out_shape=(big, big, big, big, jax.ShapeDtypeStruct((NI, NJ), F32), jax.ShapeDtypeStruct((1,), F32)),
         in_specs=[vmem] * 6 + [smem] + [vmem] * 2,
-        out_specs=(vmem,) * 5,
+        out_specs=(vmem,) * 5 + (smem,),
         scratch_shapes=[
-            pltpu.VMEM((6 * K + NI, NJ), F32), pltpu.VMEM((6 * K + NI, NJ), F32),
+            row_scratch, row_scratch,
             pltpu.VMEM((2, NI, NJ), F32), pltpu.VMEM((2, NI, NJ), F32),
-            pltpu.VMEM((6 * K + NI, NJ), F32), pltpu.VMEM((6 * K + NI, NJ), F32),
+            row_scratch, row_scratch,
             pltpu.VMEM((6, 2, NI, NJ), F32), pltpu.VMEM((6, K, NJ), F32),
+            pltpu.VMEM((2, n_half, EARLY, NI, NJ), F32), pltpu.VMEM((2, n_half, LATE, NI, NJ), F32),
+            pltpu.VMEM((3, n_lat, n_lon * NI, NJ), F32),
             pltpu.SemaphoreType.DMA((8,)), pltpu.SemaphoreType.DMA((8,)),
+            pltpu.SemaphoreType.DMA((4,)), pltpu.SemaphoreType.DMA((4,)),
         ],
         compiler_params=pltpu.CompilerParams(collective_id=0, has_side_effects=True),
         name="step",
     )(temp, salt, u, v, num, sea, thick, eta, drive)
-    gathered = lax.all_gather(packet, ("lat", "lon")).reshape(n_lat, n_lon, FIELDS, NI, NJ)
-    new_u, new_v, surface, rms = pl.pallas_call(
-        functools.partial(solve_kernel, n_lon, n_lat),
-        out_shape=(big, big, jax.ShapeDtypeStruct((NI, NJ), F32), jax.ShapeDtypeStruct((1,), F32)),
-        in_specs=[vmem] * 5,
-        out_specs=(vmem, vmem, vmem, smem),
-        scratch_shapes=[pltpu.VMEM((3, n_lat, n_lon * NI, NJ), F32)],
-        name="solve",
-    )(gathered, u_star, v_star, num, sea)
     return new_t, new_s, new_u, new_v, surface, rms.reshape(())
 
 

time: 96.7 us -> 32.9 us (0.34)
  the two profiles are of different devices: /device:TPU:0 before, /device:TPU:1 now
where the time goes in v2:
time: 32.9 us; the launch traced here: 32.7 us
  Pallas kernels  25.4 us (77%)
  local copies, waits for them, and re-layouts  4.77 us (14%)
  between operations  2.46 us (7%)
    pallas_call x1, Pallas kernels, per_device(): pl.pallas_call(functools.partial(step_kernel, n_lon, n_lat), out_shape=(b...  25.4 us
    unnamed x13, local copies, waits for them, and re-layouts  4.77 us

profile of v2, /device:TPU:1, one launch (start us, length us, event | category | flops | bytes accessed | tf_op | source)
XLA Modules:
  0.0 32.7 jit_solution(14520626509729423538)
XLA Ops:
  0.6 25.4 %step.1 = (f32[32,8,128]{2,1,0:T(8,128)}, f32[32,8,128]{2,1,0:T(8,128)}, f32[32,8,128]{2,1,0:T(8,128)}, f32[32,8,128]{2,1,0:T(8,128)}, f32[8,128]{1,0:T(8,128)}, /*index=5*/f32[1]{0:T(128)}) custom-call(f32[32,8,128]{2,1,0:T(8,128)} %t_ref.1, f32[32,8,128]{2,1,0:T(8,128)} %s_ref.1, f32[32,8,128]{2,1,0:T(8,128)} %u_ref.1, f32[32,8,128]{2,1,0:T(8,128)} %v_ref.1, ...), custom_call_target="tpu_custom_call" | custom-call | tf_op jit(solution)/shard_map/step/pallas_call | solution.py:601
  26.1 0.0 copy-start.2
  26.1 1.6 %copy.21 = f32[32,8,128]{2,1,0:T(8,128)} copy(f32[32,8,128]{2,1,0:T(8,128)} %get-tuple-element.24) | data formatting | bytes 262144
  27.7 0.0 copy-done.2
  27.7 0.0 copy-start.1
  27.7 0.7 %copy.22 = f32[32,8,128]{2,1,0:T(8,128)} copy(f32[32,8,128]{2,1,0:T(8,128)S(1)} %copy-done.2) | data formatting | bytes 262144
  28.4 0.3 copy-done.1
  28.6 0.0 copy-start
  28.7 0.7 %copy.23 = f32[32,8,128]{2,1,0:T(8,128)} copy(f32[32,8,128]{2,1,0:T(8,128)S(1)} %copy-done.1) | data formatting | bytes 262144
  29.3 0.3 copy-done
  29.6 0.0 copy-start.3
  29.6 0.7 %copy.24 = f32[32,8,128]{2,1,0:T(8,128)} copy(f32[32,8,128]{2,1,0:T(8,128)S(1)} %copy-done) | data formatting | bytes 262144
  30.3 0.0 copy-done.3
  30.3 0.6 %copy.25 = f32[8,128]{1,0:T(8,128)} copy(f32[8,128]{1,0:T(8,128)S(1)} %copy-done.3) | data formatting | bytes 8192
Async XLA Ops:
  26.1 1.6 %copy-start.2 = (f32[32,8,128]{2,1,0:T(8,128)S(1)}, f32[32,8,128]{2,1,0:T(8,128)}, u32[]{:S(2)}) copy-start(f32[32,8,128]{2,1,0:T(8,128)} %get-tuple-element.25) | copy-start | bytes 393220
  27.7 1.0 %copy-start.1 = (f32[32,8,128]{2,1,0:T(8,128)S(1)}, f32[32,8,128]{2,1,0:T(8,128)}, u32[]{:S(2)}) copy-start(f32[32,8,128]{2,1,0:T(8,128)} %get-tuple-element.26) | copy-start | bytes 393220
  28.6 1.0 %copy-start = (f32[32,8,128]{2,1,0:T(8,128)S(1)}, f32[32,8,128]{2,1,0:T(8,128)}, u32[]{:S(2)}) copy-start(f32[32,8,128]{2,1,0:T(8,128)} %get-tuple-element.27) | copy-start | bytes 393220
  29.6 0.7 %copy-start.3 = (f32[8,128]{1,0:T(8,128)S(1)}, f32[8,128]{1,0:T(8,128)}, u32[]{:S(2)}) copy-start(f32[8,128]{1,0:T(8,128)} %get-tuple-element.28) | copy-start | bytes 12292

commit v3 on v2

--- a/solution.py
+++ b/solution.py
@@ -46,10 +46,18 @@
     return x
 
 
-def step_kernel(n_lon, n_lat, t_ref, s_ref, u_ref, v_ref, num_ref, sea_ref, thick_ref, eta_ref,
-                drive_ref, ot_ref, os_ref, ou_ref, ov_ref, ox_ref, orms_ref, epk, wpk, npk, spk, slot_e,
-                slot_w, slots, rim, early, late, held, send_sem, recv_sem, cast_send, cast_recv):
+def step_kernel(n_lon, n_lat, KC, *refs):
+    sources, refs = refs[:9], refs[9:]
+    ot_ref, os_ref, ou_ref, ov_ref, ox_ref, orms_ref = refs[:6]
+    inputs, refs = refs[6:15], refs[15:]
+    t_ref, s_ref, u_ref, v_ref, num_ref, sea_ref, thick_ref, eta_ref, drive_ref = inputs
+    (epk, wpk, ebase, wbase, npk, spk, slot_e, slot_w, base_e, base_w, slots, rim, early, late, held,
+     load_sem, send_sem, recv_sem, side_send, side_recv, cast_send, cast_recv) = refs
     K, NI, NJ = t_ref.shape
+    NC = K // KC
+    loads = [pltpu.make_async_copy(src, dst, load_sem.at[i]) for i, (src, dst) in enumerate(zip(sources, inputs))]
+    for load in loads[4:] + loads[:4]:
+        load.start()
     p = lax.axis_index("lon")
     q = lax.axis_index("lat")
     east_dev = lax.rem(p + 1, n_lon)
@@ -111,6 +119,8 @@
     lax.fori_loop(1, n_half, greet_half, 0)
     greet(p, partner)
 
+    for load in loads:
+        load.wait()
     sub = iota((NI, NJ), 0)
     lane = iota((NI, NJ), 1)
     depth = (num_ref[...] * sea_ref[...]).astype(F32)
@@ -122,14 +132,12 @@
     early[parity, me_half, 2] = drive_ref[...]
 
     fields = (t_ref, s_ref, u_ref, v_ref)
-    for pk, d1, d2 in ((epk, NI - 1, NI - 2), (wpk, 0, 1)):
-        for f, ref in enumerate(fields):
-            pk[f * K:(f + 1) * K, :] = ref[:, d1, :]
-        pk[4 * K:5 * K, :] = u_ref[:, d2, :]
-        pk[5 * K:6 * K, :] = v_ref[:, d2, :]
-        pk[6 * K:6 * K + NI, :] = jnp.zeros((NI, NJ), F32)
-        pk[6 * K:6 * K + 1, :] = depth[d1:d1 + 1, :]
-        pk[6 * K + 1:6 * K + 2, :] = depth[d2:d2 + 1, :]
+    for pk, base, d1, d2 in ((epk, ebase, NI - 1, NI - 2), (wpk, wbase, 0, 1)):
+        for c in range(NC):
+            levels = slice(c * KC, (c + 1) * KC)
+            for f, (ref, d) in enumerate(((t_ref, d1), (s_ref, d1), (u_ref, d1), (v_ref, d1), (u_ref, d2), (v_ref, d2))):
+                pk[c, f * KC:(f + 1) * KC, :] = ref[levels, d, :]
+        base[...] = jnp.where(sub == 0, depth[d1:d1 + 1, :], depth[d2:d2 + 1, :])
 
     n0 = jnp.zeros((NI, NJ), F32)
     s0 = jnp.zeros((NI, NJ), F32)
@@ -162,16 +170,24 @@
 
     def copy(src, dst, lon, lat, out, into):
         return pltpu.make_async_remote_copy(
-            src_ref=src, dst_ref=dst, send_sem=send_sem.at[out], recv_sem=recv_sem.at[into],
+            src_ref=src, dst_ref=dst, send_sem=out, recv_sem=into,
             device_id={"lon": lon, "lat": lat}, device_id_type=MESH)
 
     def edge(src, slot, lon, lat, out):
-        return copy(src, slots.at[slot], lon, lat, out, slot)
-
-    to_east = copy(epk, slot_w, east_dev, q, SEM_E, SEM_W)
-    to_west = copy(wpk, slot_e, west_dev, q, SEM_W, SEM_E)
-    to_east.start()
-    to_west.start()
+        return copy(src, slots.at[slot], lon, lat, send_sem.at[out], recv_sem.at[slot])
+
+    def side_east(c):
+        return copy(epk.at[c], slot_w.at[c], east_dev, q, side_send.at[0, c], side_recv.at[0, c])
+
+    def side_west(c):
+        return copy(wpk.at[c], slot_e.at[c], west_dev, q, side_send.at[1, c], side_recv.at[1, c])
+
+    base_east = copy(ebase, base_w, east_dev, q, send_sem.at[SEM_E], recv_sem.at[SEM_W])
+    base_west = copy(wbase, base_e, west_dev, q, send_sem.at[SEM_W], recv_sem.at[SEM_E])
+    base_east.start()
+    base_west.start()
+    side_east(0).start()
+    side_west(0).start()
 
     @pl.when(not_south)
     def _():
@@ -217,6 +233,9 @@
             src_ref=buf.at[parity], dst_ref=buf.at[parity], send_sem=cast_send.at[which],
             recv_sem=cast_recv.at[which], device_id={"lon": p, "lat": partner}, device_id_type=MESH)
 
+    for c in range(1, NC):
+        side_east(c).start()
+        side_west(c).start()
     cast(early, 0)
 
     edge(npk, SLOT_N, p, q, SLOT_N).wait_recv()
@@ -286,39 +305,43 @@
     rim[4, NI:2 * NI, :] = pn0
     rim[5, NI:2 * NI, :] = ps0
 
-    to_east.wait_recv()
-    to_west.wait_recv()
-
-    level_r = iota((K, NJ), 0)
-    lane_r = iota((K, NJ), 1)
-    level_rf = level_r.astype(F32) + 0.5
-
-    def wet_r(d):
-        return jnp.where(level_rf < d, 1.0, 0.0)
+    base_east.wait_recv()
+    base_west.wait_recv()
+
+    row_c = iota((KC, NJ), 0)
+    lane_c = iota((KC, NJ), 1)
 
     def wide(row):
-        return jnp.broadcast_to(row, (K, NJ))
-
-    for side, (slot, pk, d1, cn0, cn1, cs0, cs1) in enumerate((
-            (slot_e, epk, NI - 1, pne0[0:1], pne1[0:1], pse0[0:1], pse1[0:1]),
-            (slot_w, wpk, 0, pnw0[NI - 1:], pnw1[NI - 1:], psw0[NI - 1:], psw1[NI - 1:]))):
-        d = wide(slot[6 * K:6 * K + 1, :])
-        far = wet_r(wide(slot[6 * K + 1:6 * K + 2, :]))
-        own = wet_r(wide(depth[d1:d1 + 1, :]))
-        dn = jnp.where(lane_r == NJ - 1, jnp.broadcast_to(cn1[:, 0:1], (K, NJ)), pltpu.roll(d, NJ - 1, 1))
-        ds = jnp.where(lane_r == 0, jnp.broadcast_to(cs1[:, 0:1], (K, NJ)), pltpu.roll(d, 1, 1))
-        mid, mn, ms = wet_r(d), wet_r(dn), wet_r(ds)
-        for i in range(2):
-            f = 2 + i
-            x = slot[f * K:(f + 1) * K, :]
-            pick = lane_r == level_r + f * K
-            cn = jnp.sum(jnp.where(pick, wide(cn0), 0.0), axis=1, keepdims=True)
-            cs = jnp.sum(jnp.where(pick, wide(cs0), 0.0), axis=1, keepdims=True)
-            xn = jnp.where(lane_r == NJ - 1, jnp.broadcast_to(cn, (K, NJ)), pltpu.roll(x, NJ - 1, 1))
-            xs = jnp.where(lane_r == 0, jnp.broadcast_to(cs, (K, NJ)), pltpu.roll(x, 1, 1))
-            total = far * (slot[(4 + i) * K:(5 + i) * K, :] - x) + own * (pk[f * K:(f + 1) * K, :] - x)
-            total = total + mn * (xn - x) + ms * (xs - x)
-            rim[2 * side + i] = mid * total
+        return jnp.broadcast_to(row, (KC, NJ))
+
+    rim[6, 0:NI, :] = pne0
+    rim[6, NI:2 * NI, :] = pse0
+    rim[7, 0:NI, :] = pnw0
+    rim[7, NI:2 * NI, :] = psw0
+    side_depths = []
+    for base, d1, cn1, cs1 in ((base_e, NI - 1, pne1[0:1], pse1[0:1]), (base_w, 0, pnw1[NI - 1:], psw1[NI - 1:])):
+        d = wide(base[0:1, :])
+        dn = jnp.where(lane_c == NJ - 1, jnp.broadcast_to(cn1[:, 0:1], (KC, NJ)), pltpu.roll(d, NJ - 1, 1))
+        ds = jnp.where(lane_c == 0, jnp.broadcast_to(cs1[:, 0:1], (KC, NJ)), pltpu.roll(d, 1, 1))
+        side_depths.append((d, wide(base[1:2, :]), wide(depth[d1:d1 + 1, :]), dn, ds))
+
+    def side_laps(c):
+        level_c = (row_c + c * KC).astype(F32) + 0.5
+        for side, (slot, pk, corner) in enumerate(((slot_e, epk, 0), (slot_w, wpk, NI - 1))):
+            mid, far, own, mn, ms = [jnp.where(level_c < d, 1.0, 0.0) for d in side_depths[side]]
+            cn0 = rim[6 + side, corner:corner + 1, :]
+            cs0 = rim[6 + side, NI + corner:NI + corner + 1, :]
+            for i in range(2):
+                f = 2 + i
+                x = slot[c, f * KC:(f + 1) * KC, :]
+                pick = lane_c == row_c + (c * KC + f * K)
+                cn = jnp.sum(jnp.where(pick, wide(cn0), 0.0), axis=1, keepdims=True)
+                cs = jnp.sum(jnp.where(pick, wide(cs0), 0.0), axis=1, keepdims=True)
+                xn = jnp.where(lane_c == NJ - 1, jnp.broadcast_to(cn, (KC, NJ)), pltpu.roll(x, NJ - 1, 1))
+                xs = jnp.where(lane_c == 0, jnp.broadcast_to(cs, (KC, NJ)), pltpu.roll(x, 1, 1))
+                total = far * (slot[c, (4 + i) * KC:(5 + i) * KC, :] - x)
+                total = total + own * (pk[c, f * KC:(f + 1) * KC, :] - x) + mn * (xn - x) + ms * (xs - x)
+                rim[2 * side + i, 0:KC, :] = mid * total
 
     def shift_n(x, packed, source):
         return jnp.where(lane == NJ - 1, pltpu.roll(packed, NJ - 1 - source, 1), pltpu.roll(x, NJ - 1, 1))
@@ -326,8 +349,8 @@
     def shift_s(x, packed, source):
         return jnp.where(lane == 0, pltpu.roll(packed, lax.rem(NJ - source, NJ), 1), pltpu.roll(x, 1, 1))
 
-    depth_e = shift_e(depth, slot_e[6 * K:6 * K + 1, :])
-    depth_w = shift_w(depth, slot_w[6 * K:6 * K + 1, :])
+    depth_e = shift_e(depth, base_e[0:1, :])
+    depth_w = shift_w(depth, base_w[0:1, :])
     depth_n = shift_n(depth, pn1, 0)
     depth_s = jnp.where(lane == 0, ps1, pltpu.roll(depth, 1, 1))
     both_e = jnp.minimum(depth, depth_e)
@@ -339,7 +362,9 @@
 
     zero = jnp.zeros((NI, NJ), F32)
 
-    def level(k, carry):
+    def level(c, i, carry):
+        k = c * KC + i
+        inner = i
         pc, pe, pw, pn_, ps_, flux_t, flux_s, tu, tv = carry
         kf = lax.convert_element_type(k, F32) + 0.5
         h = thick_ref[k]
@@ -362,8 +387,8 @@
 
         def around(ref, f):
             x = ref[k]
-            row = pl.ds(f * K + k, 1)
-            return (x, shift_e(x, slot_e[row, :]), shift_w(x, slot_w[row, :]),
+            row = f * KC + inner
+            return (x, shift_e(x, slot_e[c, row:row + 1, :]), shift_w(x, slot_w[c, row:row + 1, :]),
                     shift_n(x, pn0v, f * K + k), shift_s(x, ps0v, f * K + k))
 
         t = around(t_ref, 0)
@@ -398,9 +423,8 @@
         def biharmonic(x, i):
             c, e, w, n, so = x
             lap = me * (e - c) + mw * (w - c) + mn * (n - c) + ms * (so - c)
-            row = pl.ds(k, 1)
-            le = shift_e(lap, rim[i, row, :])
-            lw = shift_w(lap, rim[2 + i, row, :])
+            le = shift_e(lap, rim[i, inner:inner + 1, :])
+            lw = shift_w(lap, rim[2 + i, inner:inner + 1, :])
             source = (2 + i) * K + k
             ln = shift_n(lap, lapn, source)
             ls = shift_s(lap, laps, source)
@@ -412,14 +436,15 @@
         ov_ref[k] = v_star
         return (pc, pe, pw, pn_, ps_, flux_t, flux_s, tu + h * u_star, tv + h * v_star)
 
-    unroll = 4 if K % 4 == 0 else 1
-
-    def group(g, carry):
-        for i in range(unroll):
-            carry = level(g * unroll + i, carry)
+    def chunk(c, carry):
+        side_east(c).wait_recv()
+        side_west(c).wait_recv()
+        side_laps(c)
+        for i in range(KC):
+            carry = level(c, i, carry)
         return carry
 
-    carry = lax.fori_loop(0, K // unroll, group, (zero,) * 9)
+    carry = lax.fori_loop(0, NC, chunk, (zero,) * 9)
     late[parity, me_half, 0] = carry[7]
     late[parity, me_half, 1] = carry[8]
     cast(late, 1)
@@ -453,21 +478,20 @@
                 held[i, b, pl.ds(s, n_lon, stride=NI), :] = field[b][s]
     orms_ref[0] = jnp.max(jnp.broadcast_to(rms, (8, 128)))
     block = pl.ds(pl.multiple_of(p * NI, NI), NI)
-    ox_ref[...] = held[0, q, block, :]
-    su = GRAVITY * held[1, q, block, :]
-    sv = GRAVITY * held[2, q, block, :]
-    for k in range(K):
-        wet = depth > k + 0.5
-        ou_ref[k] = jnp.where(wet, ou_ref[k] - su, 0.0)
-        ov_ref[k] = jnp.where(wet, ov_ref[k] - sv, 0.0)
+    ox_ref[0] = held[0, q, block, :]
+    ox_ref[1] = GRAVITY * held[1, q, block, :]
+    ox_ref[2] = GRAVITY * held[2, q, block, :]
 
     cast_wait(early, cast_send.at[0])
     cast_wait(late, cast_send.at[1])
     early_over.wait_send()
     hand_over(late, 3).wait_send()
 
-    to_east.wait_send()
-    to_west.wait_send()
+    base_east.wait_send()
+    base_west.wait_send()
+    for c in range(NC):
+        side_east(c).wait_send()
+        side_west(c).wait_send()
 
     @pl.when(not_south)
     def _():
@@ -591,32 +615,65 @@
     return x, slope_x, slope_y, rms
 
 
+def finish_kernel(t_ref, s_ref, u_ref, v_ref, x_ref, rms_ref, num_ref, sea_ref, ot_ref, os_ref, ou_ref,
+                  ov_ref, ox_ref, orms_ref):
+    depth = (num_ref[...] * sea_ref[...]).astype(F32)
+    su = x_ref[1]
+    sv = x_ref[2]
+    for k in range(t_ref.shape[0]):
+        wet = depth > k + 0.5
+        ot_ref[k] = t_ref[k]
+        os_ref[k] = s_ref[k]
+        ou_ref[k] = jnp.where(wet, u_ref[k] - su, 0.0)
+        ov_ref[k] = jnp.where(wet, v_ref[k] - sv, 0.0)
+    ox_ref[...] = x_ref[0]
+    orms_ref[0] = rms_ref[0]
+
+
 def per_device(n_lon, n_lat, temp, salt, u, v, num, sea, thick, eta, drive):
     K, NI, NJ = temp.shape
+    KC = 8 if K % 8 == 0 else K
+    NC = K // KC
+    n_half = n_lon * n_lat // 2
     vmem = pl.BlockSpec(memory_space=pltpu.VMEM)
     smem = pl.BlockSpec(memory_space=pltpu.SMEM)
+    anywhere = pl.BlockSpec(memory_space=pltpu.HBM)
     big = jax.ShapeDtypeStruct((K, NI, NJ), F32)
-    n_half = n_lon * n_lat // 2
-    row_scratch = pltpu.VMEM((6 * K + NI, NJ), F32)
-    new_t, new_s, new_u, new_v, surface, rms = pl.pallas_call(
-        functools.partial(step_kernel, n_lon, n_lat),
-        out_shape=(big, big, big, big, jax.ShapeDtypeStruct((NI, NJ), F32), jax.ShapeDtypeStruct((1,), F32)),
-        in_specs=[vmem] * 6 + [smem] + [vmem] * 2,
+    flat = jax.ShapeDtypeStruct((NI, NJ), F32)
+    one = jax.ShapeDtypeStruct((1,), F32)
+    args = (temp, salt, u, v, num, sea, thick, eta, drive)
+    sides = pltpu.VMEM((NC, 6 * KC, NJ), F32)
+    tile = pltpu.VMEM((NI, NJ), F32)
+    parts = pl.pallas_call(
+        functools.partial(step_kernel, n_lon, n_lat, KC),
+        out_shape=(big, big, big, big, jax.ShapeDtypeStruct((3, NI, NJ), F32), one),
+        in_specs=[anywhere] * 9,
         out_specs=(vmem,) * 5 + (smem,),
-        scratch_shapes=[
-            row_scratch, row_scratch,
+        scratch_shapes=[(pltpu.SMEM if a.ndim == 1 else pltpu.VMEM)(a.shape, a.dtype) for a in args] + [
+            sides, sides, tile, tile,
             pltpu.VMEM((2, NI, NJ), F32), pltpu.VMEM((2, NI, NJ), F32),
-            row_scratch, row_scratch,
-            pltpu.VMEM((6, 2, NI, NJ), F32), pltpu.VMEM((6, K, NJ), F32),
+            sides, sides, tile, tile,
+            pltpu.VMEM((6, 2, NI, NJ), F32), pltpu.VMEM((8, max(KC, 2 * NI), NJ), F32),
             pltpu.VMEM((2, n_half, EARLY, NI, NJ), F32), pltpu.VMEM((2, n_half, LATE, NI, NJ), F32),
             pltpu.VMEM((3, n_lat, n_lon * NI, NJ), F32),
+            pltpu.SemaphoreType.DMA((9,)),
             pltpu.SemaphoreType.DMA((8,)), pltpu.SemaphoreType.DMA((8,)),
+            pltpu.SemaphoreType.DMA((2, NC)), pltpu.SemaphoreType.DMA((2, NC)),
             pltpu.SemaphoreType.DMA((4,)), pltpu.SemaphoreType.DMA((4,)),
         ],
-        compiler_params=pltpu.CompilerParams(collective_id=0, has_side_effects=True),
+        compiler_params=pltpu.CompilerParams(
+            collective_id=0, has_side_effects=True, vmem_limit_bytes=40 * 1024 * 1024),
         name="step",
-    )(temp, salt, u, v, num, sea, thick, eta, drive)
-    return new_t, new_s, new_u, new_v, surface, rms.reshape(())
+    )(*args)
+    outs = pl.pallas_call(
+        finish_kernel,
+        out_shape=(big, big, big, big, flat, one),
+        in_specs=[vmem] * 5 + [smem] + [vmem] * 2,
+        out_specs=(vmem,) * 5 + (smem,),
+        compiler_params=pltpu.CompilerParams(vmem_limit_bytes=16 * 1024 * 1024),
+        name="finish",
+    )(*parts, num, sea)
+    return outs[:5] + (outs[5].reshape(()),)
 
 
 def solution(mesh):

time: 32.9 us -> 33.1 us (level)
  local copies, waits for them, and re-layouts: 4.77 us -> 7.01 us
  between operations: 2.46 us -> 0.66 us
    unnamed x13 -> x18, local copies, waits for them, and re-layouts: 4.77 us -> 7.01 us
    pallas_call x1 -> x2, Pallas kernels: 25.4 us -> 25.1 us  [the longest x1 23.6 us: per_device(): pl.pallas_call(functools.partial(step_kernel, n_lon, n_lat, KC), out_shap...]
where the time goes in v3:
time: 33.1 us; the launch traced here: 32.8 us
  Pallas kernels  25.1 us (76%)
  local copies, waits for them, and re-layouts  7.01 us (21%)
  between operations  0.66 us (2%)
    pallas_call x1, Pallas kernels, per_device(): pl.pallas_call(functools.partial(step_kernel, n_lon, n_lat, KC), out_shap...  23.6 us
    unnamed x18, local copies, waits for them, and re-layouts  7.01 us
    pallas_call x1, Pallas kernels, per_device(): pl.pallas_call(finish_kernel, out_shape=(big, big, big, big, flat, one),...  1.46 us

profile of v3, /device:TPU:1, one launch (start us, length us, event | category | flops | bytes accessed | tf_op | source)
XLA Modules:
  0.0 32.8 jit_solution(1071651555283423142)
XLA Ops:
  0.6 0.0 copy-start
  0.6 0.9 %copy-done = f32[32,8,128]{2,1,0:T(8,128)S(1)} copy-done((f32[32,8,128]{2,1,0:T(8,128)S(1)}, f32[32,8,128]{2,1,0:T(8,128)}, u32[]{:S(2)}) %copy-start) | copy-done | bytes 131096
  1.5 0.0 copy-start.1
  1.5 0.9 %copy-done.1 = f32[32,8,128]{2,1,0:T(8,128)S(1)} copy-done((f32[32,8,128]{2,1,0:T(8,128)S(1)}, f32[32,8,128]{2,1,0:T(8,128)}, u32[]{:S(2)}) %copy-start.1) | copy-done | bytes 131096
  2.4 0.0 copy-start.2
  2.4 0.9 %copy-done.2 = f32[32,8,128]{2,1,0:T(8,128)S(1)} copy-done((f32[32,8,128]{2,1,0:T(8,128)S(1)}, f32[32,8,128]{2,1,0:T(8,128)}, u32[]{:S(2)}) %copy-start.2) | copy-done | bytes 131096
  3.4 0.0 copy-start.3
  3.4 0.9 %copy-done.3 = f32[32,8,128]{2,1,0:T(8,128)S(1)} copy-done((f32[32,8,128]{2,1,0:T(8,128)S(1)}, f32[32,8,128]{2,1,0:T(8,128)}, u32[]{:S(2)}) %copy-start.3) | copy-done | bytes 131096
  4.3 0.0 copy-start.4
  4.3 0.7 %copy-done.4 = s32[8,128]{1,0:T(8,128)S(1)} copy-done((s32[8,128]{1,0:T(8,128)S(1)}, s32[8,128]{1,0:T(8,128)}, u32[]{:S(2)}) %copy-start.4) | copy-done | bytes 4120
  4.9 0.0 copy-start.5
  4.9 0.7 %copy-done.5 = s32[8,128]{1,0:T(8,128)S(1)} copy-done((s32[8,128]{1,0:T(8,128)S(1)}, s32[8,128]{1,0:T(8,128)}, u32[]{:S(2)}) %copy-start.5) | copy-done | bytes 4120
  5.6 0.0 copy-start.6
  5.6 0.7 %copy-done.6 = f32[8,128]{1,0:T(8,128)S(1)} copy-done((f32[8,128]{1,0:T(8,128)S(1)}, f32[8,128]{1,0:T(8,128)}, u32[]{:S(2)}) %copy-start.6) | copy-done | bytes 4120
  6.3 0.0 copy-start.7
  6.3 0.7 %copy-done.7 = f32[8,128]{1,0:T(8,128)S(1)} copy-done((f32[8,128]{1,0:T(8,128)S(1)}, f32[8,128]{1,0:T(8,128)}, u32[]{:S(2)}) %copy-start.7) | copy-done | bytes 4120
  7.0 0.0 copy-start.8
  7.0 0.7 %copy-done.8 = f32[32]{0:T(128)S(1)} copy-done((f32[32]{0:T(128)S(1)}, f32[32]{0:T(128)}, u32[]{:S(2)}) %copy-start.8) | copy-done | bytes 152
  7.7 23.6 %step.1 = (f32[32,8,128]{2,1,0:T(8,128)S(1)}, f32[32,8,128]{2,1,0:T(8,128)S(1)}, f32[32,8,128]{2,1,0:T(8,128)S(1)}, f32[32,8,128]{2,1,0:T(8,128)S(1)}, f32[3,8,128]{2,1,0:T(8,128)S(1)}, /*index=5*/f32[1]{0:T(128)}) custom-call(f32[32,8,128]{2,1,0:T(8,128)S(1)} %copy-done, f32[32,8,128]{2,1,0:T(8,128)S(1)} %copy-done.1, f32[32,8,128]{2,1,0:T(8,128)S(1)} %copy-done.2, ...), custom_call_target="tpu_custom_call" | custom-call | tf_op jit(solution)/shard_map/step/pallas_call | solution.py:647
  31.3 1.5 %finish.1 = (f32[32,8,128]{2,1,0:T(8,128)}, f32[32,8,128]{2,1,0:T(8,128)}, f32[32,8,128]{2,1,0:T(8,128)}, f32[32,8,128]{2,1,0:T(8,128)}, f32[8,128]{1,0:T(8,128)}, /*index=5*/f32[1]{0:T(128)}) custom-call(f32[32,8,128]{2,1,0:T(8,128)S(1)} %get-tuple-element.18.t_ref, f32[32,8,128]{2,1,0:T(8,128)S(1)} %get-tuple-element.19.s_ref, ...), custom_call_target="tpu_custom_call" | custom-call | tf_op jit(solution)/shard_map/finish/pallas_call | solution.py:668
Async XLA Ops:
  0.6 0.9 %copy-start = (f32[32,8,128]{2,1,0:T(8,128)S(1)}, f32[32,8,128]{2,1,0:T(8,128)}, u32[]{:S(2)}) copy-start(f32[32,8,128]{2,1,0:T(8,128)} %refs_0_.1) | copy-start | bytes 393220
  1.5 0.9 %copy-start.1 = (f32[32,8,128]{2,1,0:T(8,128)S(1)}, f32[32,8,128]{2,1,0:T(8,128)}, u32[]{:S(2)}) copy-start(f32[32,8,128]{2,1,0:T(8,128)} %refs_1_.1) | copy-start | bytes 393220
  2.4 0.9 %copy-start.2 = (f32[32,8,128]{2,1,0:T(8,128)S(1)}, f32[32,8,128]{2,1,0:T(8,128)}, u32[]{:S(2)}) copy-start(f32[32,8,128]{2,1,0:T(8,128)} %refs_2_.1) | copy-start | bytes 393220
  3.4 0.9 %copy-start.3 = (f32[32,8,128]{2,1,0:T(8,128)S(1)}, f32[32,8,128]{2,1,0:T(8,128)}, u32[]{:S(2)}) copy-start(f32[32,8,128]{2,1,0:T(8,128)} %refs_3_.1) | copy-start | bytes 393220
  4.3 0.7 %copy-start.4 = (s32[8,128]{1,0:T(8,128)S(1)}, s32[8,128]{1,0:T(8,128)}, u32[]{:S(2)}) copy-start(s32[8,128]{1,0:T(8,128)} %num_ref.1) | copy-start | bytes 12292
  4.9 0.7 %copy-start.5 = (s32[8,128]{1,0:T(8,128)S(1)}, s32[8,128]{1,0:T(8,128)}, u32[]{:S(2)}) copy-start(s32[8,128]{1,0:T(8,128)} %sea_ref.1) | copy-start | bytes 12292
  5.6 0.7 %copy-start.6 = (f32[8,128]{1,0:T(8,128)S(1)}, f32[8,128]{1,0:T(8,128)}, u32[]{:S(2)}) copy-start(f32[8,128]{1,0:T(8,128)} %refs_7_.1) | copy-start | bytes 12292
  6.3 0.7 %copy-start.7 = (f32[8,128]{1,0:T(8,128)S(1)}, f32[8,128]{1,0:T(8,128)}, u32[]{:S(2)}) copy-start(f32[8,128]{1,0:T(8,128)} %refs_8_.1) | copy-start | bytes 12292
  7.0 0.7 %copy-start.8 = (f32[32]{0:T(128)S(1)}, f32[32]{0:T(128)}, u32[]{:S(2)}) copy-start(f32[32]{0:T(128)} %refs_6_.1) | copy-start | bytes 388

commit v4 on v3

--- a/solution.py
+++ b/solution.py
@@ -48,11 +48,11 @@
 
 def step_kernel(n_lon, n_lat, KC, *refs):
     sources, refs = refs[:9], refs[9:]
-    ot_ref, os_ref, ou_ref, ov_ref, ox_ref, orms_ref = refs[:6]
+    targets, (ox_ref, orms_ref) = refs[:4], refs[4:6]
     inputs, refs = refs[6:15], refs[15:]
     t_ref, s_ref, u_ref, v_ref, num_ref, sea_ref, thick_ref, eta_ref, drive_ref = inputs
     (epk, wpk, ebase, wbase, npk, spk, slot_e, slot_w, base_e, base_w, slots, rim, early, late, held,
-     load_sem, send_sem, recv_sem, side_send, side_recv, cast_send, cast_recv) = refs
+     ot_ref, os_ref, ou_ref, ov_ref, load_sem, store_sem, send_sem, recv_sem, side_send, side_recv, cast_send, cast_recv) = refs
     K, NI, NJ = t_ref.shape
     NC = K // KC
     loads = [pltpu.make_async_copy(src, dst, load_sem.at[i]) for i, (src, dst) in enumerate(zip(sources, inputs))]
@@ -448,6 +448,10 @@
     late[parity, me_half, 0] = carry[7]
     late[parity, me_half, 1] = carry[8]
     cast(late, 1)
+    stores = [pltpu.make_async_copy(src, dst, store_sem.at[i])
+              for i, (src, dst) in enumerate(zip((ot_ref, os_ref, ou_ref, ov_ref), targets))]
+    for store in stores:
+        store.start()
 
     cast_wait(early, cast_recv.at[0])
     early_over = hand_over(early, 2)
@@ -482,6 +486,8 @@
     ox_ref[1] = GRAVITY * held[1, q, block, :]
     ox_ref[2] = GRAVITY * held[2, q, block, :]
 
+    for store in stores:
+        store.wait()
     cast_wait(early, cast_send.at[0])
     cast_wait(late, cast_send.at[1])
     early_over.wait_send()
@@ -648,7 +654,7 @@
         functools.partial(step_kernel, n_lon, n_lat, KC),
         out_shape=(big, big, big, big, jax.ShapeDtypeStruct((3, NI, NJ), F32), one),
         in_specs=[anywhere] * 9,
-        out_specs=(vmem,) * 5 + (smem,),
+        out_specs=(anywhere,) * 4 + (vmem, smem),
         scratch_shapes=[(pltpu.SMEM if a.ndim == 1 else pltpu.VMEM)(a.shape, a.dtype) for a in args] + [
             sides, sides, tile, tile,
             pltpu.VMEM((2, NI, NJ), F32), pltpu.VMEM((2, NI, NJ), F32),
@@ -656,13 +662,15 @@
             pltpu.VMEM((6, 2, NI, NJ), F32), pltpu.VMEM((8, max(KC, 2 * NI), NJ), F32),
             pltpu.VMEM((2, n_half, EARLY, NI, NJ), F32), pltpu.VMEM((2, n_half, LATE, NI, NJ), F32),
             pltpu.VMEM((3, n_lat, n_lon * NI, NJ), F32),
-            pltpu.SemaphoreType.DMA((9,)),
+            pltpu.VMEM((K, NI, NJ), F32), pltpu.VMEM((K, NI, NJ), F32),
+            pltpu.VMEM((K, NI, NJ), F32), pltpu.VMEM((K, NI, NJ), F32),
+            pltpu.SemaphoreType.DMA((9,)), pltpu.SemaphoreType.DMA((4,)),
             pltpu.SemaphoreType.DMA((8,)), pltpu.SemaphoreType.DMA((8,)),
             pltpu.SemaphoreType.DMA((2, NC)), pltpu.SemaphoreType.DMA((2, NC)),
             pltpu.SemaphoreType.DMA((4,)), pltpu.SemaphoreType.DMA((4,)),
         ],
         compiler_params=pltpu.CompilerParams(
-            collective_id=0, has_side_effects=True, vmem_limit_bytes=40 * 1024 * 1024),
+            collective_id=0, has_side_effects=True),
         name="step",
     )(*args)
     outs = pl.pallas_call(
@@ -670,7 +678,6 @@
         out_shape=(big, big, big, big, flat, one),
         in_specs=[vmem] * 5 + [smem] + [vmem] * 2,
         out_specs=(vmem,) * 5 + (smem,),
-        compiler_params=pltpu.CompilerParams(vmem_limit_bytes=16 * 1024 * 1024),
         name="finish",
     )(*parts, num, sea)
     return outs[:5] + (outs[5].reshape(()),)

time: 33.1 us -> 26.4 us (0.80)
  local copies, waits for them, and re-layouts: 7.01 us -> 0 us
  Pallas kernels: 25.1 us -> 25.6 us
    unnamed x18 -> x0, local copies, waits for them, and re-layouts: 7.01 us -> none
    pallas_call x1, Pallas kernels: 1.46 us -> 2.54 us  [per_device(): pl.pallas_call(finish_kernel, out_shape=(big, big, big, big, flat, one),...]
    pallas_call x1, Pallas kernels: 23.6 us -> 23 us  [per_device(): pl.pallas_call(functools.partial(step_kernel, n_lon, n_lat, KC), out_shap...]
where the time goes in v4:
time: 26.4 us; the launch traced here: 26.2 us
  Pallas kernels  25.6 us (97%)
  between operations  0.64 us (2%)
    pallas_call x1, Pallas kernels, per_device(): pl.pallas_call(functools.partial(step_kernel, n_lon, n_lat, KC), out_shap...  23 us
    pallas_call x1, Pallas kernels, per_device(): pl.pallas_call(finish_kernel, out_shape=(big, big, big, big, flat, one),...  2.54 us

profile of v4, /device:TPU:1, one launch (start us, length us, event | category | flops | bytes accessed | tf_op | source)
XLA Modules:
  0.0 26.2 jit_solution(13040796474001874340)
XLA Ops:
  0.6 23.0 %step.1 = (f32[32,8,128]{2,1,0:T(8,128)}, f32[32,8,128]{2,1,0:T(8,128)}, f32[32,8,128]{2,1,0:T(8,128)}, f32[32,8,128]{2,1,0:T(8,128)}, f32[3,8,128]{2,1,0:T(8,128)}, /*index=5*/f32[1]{0:T(128)}) custom-call(f32[32,8,128]{2,1,0:T(8,128)} %refs_0_.1, f32[32,8,128]{2,1,0:T(8,128)} %refs_1_.1, f32[32,8,128]{2,1,0:T(8,128)} %refs_2_.1, f32[32,8,128]{2,1,0:T(8,128)} %refs_3_.1, ...), custom_call_target="tpu_custom_call" | custom-call | tf_op jit(solution)/shard_map/step/pallas_call | solution.py:653
  23.7 2.5 %finish.1 = (f32[32,8,128]{2,1,0:T(8,128)}, f32[32,8,128]{2,1,0:T(8,128)}, f32[32,8,128]{2,1,0:T(8,128)}, f32[32,8,128]{2,1,0:T(8,128)}, f32[8,128]{1,0:T(8,128)}, /*index=5*/f32[1]{0:T(128)}) custom-call(f32[32,8,128]{2,1,0:T(8,128)} %get-tuple-element.18.t_ref, f32[32,8,128]{2,1,0:T(8,128)} %get-tuple-element.19.s_ref, ...), custom_call_target="tpu_custom_call" | custom-call | tf_op jit(solution)/shard_map/finish/pallas_call | solution.py:676
